TPU v7x, 512 devices: a whole 4x4x16 slice. The times are simulated.
512 devices in a mesh: rows: 128 (over z, x, core), cols: 4 (over y).
Axes of the slice: x: 4, y: 4, z: 16, core: 2. Of those that a mesh axis runs over, the one named last changes fastest.
Arguments:
- basis_rows: bfloat16 [327680, 512], P('rows', 'cols'), may hold values from -24 to 24
- stiff_blocks: bfloat16 [2560, 3, 128, 128], P('rows'), may hold values from -0.3125 to 0.3125
- block_neighbors: int32 [2560, 3], P('rows'), may hold values from 0 to 2559, as said below
- vertex_mass: float32 [327680], P('rows'), may hold values from 0.4 to 7.5
- rotation: bfloat16 [512, 512], replicated, may hold values from -0.25 to 0.25
Outputs:
- new_basis: bfloat16 [327680, 512], P('rows', 'cols')
- stiff_image: bfloat16 [327680, 512], P('rows', 'cols')
- stiff_gram: float32 [512, 512], P('rows', 'cols')
- mass_gram: float32 [512, 512], P('rows', 'cols')
Inputs may be any that keep to these rules, and one draw needn't show every extreme that they name: `block_neighbors`: entry 0 of block row b is b itself; every entry of block row b lies within 8 of b.
All inputs are finite; a program needn't handle non-finite values.
Results may differ from a plain program's by a relative error of at most 0.008.
Values may be sent and summed in bfloat16 or wider, within the bound.
A program may use at most 64 MiB of HBM per device.

v0:
```python
import jax
import jax.numpy as jnp
from jax import lax
from jax.sharding import Mesh
from jax.sharding import PartitionSpec as P

BAND = 8
ROWS = ("rows_0", "rows_1", "rows_2")


def with_halo(block, sides, width):
    for axis, dim in sides:
        count = lax.axis_size(axis)
        forward = [(i, i + 1) for i in range(count - 1)]
        backward = [(target, source) for source, target in forward]
        low = lax.ppermute(
            lax.slice_in_dim(block, block.shape[dim] - width, None, axis=dim), axis, forward
        )
        high = lax.ppermute(lax.slice_in_dim(block, 0, width, axis=dim), axis, backward)
        block = jnp.concatenate([low, block, high], axis=dim)
    return block


def from_everyone(value, axis):
    size = lax.axis_size(axis)
    return lax.all_to_all(
        jnp.broadcast_to(value[None], (size, *value.shape)), axis, 0, 0, tiled=True
    )


def laid_out(tiles, dim):
    shape = list(tiles.shape[1:])
    shape[dim] *= tiles.shape[0]
    return jnp.moveaxis(tiles, 0, dim).reshape(shape)


def gather_directly(value, axis, dim):
    tiles = from_everyone(value, axis)
    return laid_out(tiles, dim)


def cut_along(value, dim, size):
    shape = value.shape
    tiles = value.reshape(*shape[:dim], size, shape[dim] // size, *shape[dim + 1 :])
    return jnp.moveaxis(tiles, dim, 0)


def sent_and_summed(value, axis, dim):
    size = lax.axis_size(axis)
    tiles = lax.all_to_all(cut_along(value, dim, size), axis, 0, 0, tiled=True)
    return jnp.sum(tiles, axis=0)


def summed_rows(value, axes, dim):
    far, near = axes
    tiles = cut_along(value, dim, lax.axis_size(far))
    nearer = sent_and_summed(tiles, near, dim + 1)
    arrived = lax.all_to_all(nearer, far, split_axis=0, concat_axis=0, tiled=True)
    return arrived.sum(axis=0)


def taken_together(value, axis):
    everything = from_everyone(value, axis)
    return jnp.sum(everything, axis=0)


def one_axis_at_a_time(value, axes):
    far, near = axes
    return taken_together(taken_together(value, near), far)


def split_parts(values):
    high = values.astype(jnp.bfloat16)
    low = (values - high.astype(jnp.float32)).astype(jnp.bfloat16)
    return (high, low)


def apply_blocks(padded, stiff_blocks, block_neighbors, first_block, precise):
    block_count = stiff_blocks.shape[0]
    block_size = stiff_blocks.shape[2]
    col_width = padded.shape[1]
    tiles = padded.reshape(block_count + 2 * BAND, block_size, col_width)
    local_index = block_neighbors - first_block + BAND
    source = tiles[local_index]
    if precise:
        high, low = split_parts(source)
        result = jnp.einsum(
            "knij,knjc->kic", stiff_blocks, high, preferred_element_type=jnp.float32
        )
        result = result + jnp.einsum(
            "knij,knjc->kic", stiff_blocks, low, preferred_element_type=jnp.float32
        )
    else:
        result = jnp.einsum(
            "knij,knjc->kic", stiff_blocks, source, preferred_element_type=jnp.float32
        )
    return result.reshape(block_count * block_size, col_width)


def body(basis_rows, stiff_blocks, block_neighbors, vertex_mass, rotation):
    row_count = lax.axis_size(ROWS)
    row_place = lax.axis_index(ROWS)
    col_place = lax.axis_index("cols")
    local_rows, col_width = basis_rows.shape
    block_count = stiff_blocks.shape[0]
    block_size = stiff_blocks.shape[2]
    vertices = local_rows * row_count
    first_block = row_place * block_count
    local_turn = lax.dynamic_slice_in_dim(rotation, col_place * col_width, col_width, 1)
    padded = with_halo(basis_rows, ((ROWS, 0),), BAND * block_size)
    stiff_rows = apply_blocks(padded, stiff_blocks, block_neighbors, first_block, False)
    half_image = stiff_rows.astype(jnp.bfloat16)
    weighted = (vertex_mass[:, None] * basis_rows.astype(jnp.float32)).astype(jnp.bfloat16)
    piece = gather_directly(basis_rows, "cols", 1)
    turned_part = jnp.dot(piece, local_turn, preferred_element_type=jnp.float32)
    stiff_part = lax.dot_general(
        piece, half_image, (((0,), (0,)), ((), ())), preferred_element_type=jnp.float32
    )
    mass_part = lax.dot_general(
        piece, weighted, (((0,), (0,)), ((), ())), preferred_element_type=jnp.float32
    )
    grams = summed_rows(
        jnp.concatenate([stiff_part, mass_part], axis=1) / vertices,
        (("rows_0", "rows_1"), "rows_2"),
        0,
    )
    squares = jnp.sum(vertex_mass[:, None] * turned_part * turned_part, axis=0) / vertices
    scale = lax.rsqrt(one_axis_at_a_time(squares, (("rows_0", "rows_1"), "rows_2")))
    new_basis = (turned_part * scale).astype(jnp.bfloat16)
    source_rows = turned_part * scale
    rimmed = with_halo(source_rows, ((ROWS, 0),), BAND * block_size)
    product = apply_blocks(rimmed, stiff_blocks, block_neighbors, first_block, True)
    return (new_basis, product.astype(jnp.bfloat16), grams[:, :col_width], grams[:, col_width:])


def solution(mesh):
    split = Mesh(
        mesh.devices.reshape(16, 4, 2, mesh.shape["cols"]), ("rows_0", "rows_1", "rows_2", "cols")
    )
    in_specs = (P(ROWS, "cols"), P(ROWS, None, None, None), P(ROWS, None), P(ROWS), P())
    out_specs = (P(ROWS, "cols"), P(ROWS, "cols"), P(ROWS, "cols"), P(ROWS, "cols"))
    return jax.shard_map(body, mesh=split, in_specs=in_specs, out_specs=out_specs, check_vma=False)
```

profile of v0, /device:TPU:1, one launch (start us, length us, event | category | flops | bytes accessed | tf_op | source)
XLA Modules:
  0.0 135.9 jit_solution(8890763762225024918)
XLA Ops:
  0.6 0.0 copy-start
  0.6 1.5 %copy.36 = bf16[2560,128]{0,1:T(8,128)(2,1)S(1)} copy(bf16[2560,128]{1,0:T(8,128)(2,1)} %param.5) | data formatting | bytes 1310720 | tf_op args[0]
  2.1 0.0 copy-start.2
  2.1 1.7 %broadcast_in_dim.8 = bf16[4,2560,128]{1,2,0:T(8,128)(2,1)} broadcast(bf16[2560,128]{0,1:T(8,128)(2,1)S(1)} %copy.36), dimensions={1,2} | broadcast | bytes 3276800 | tf_op jit(solution)/shard_map/broadcast_in_dim | solution.py:27
  3.8 0.0 copy-start.3
  3.8 0.0 copy-start.7
  3.8 0.0 copy-done.2
  3.8 5.1 %all-to-all-start = ((bf16[4,2560,128]{1,2,0:T(8,128)(2,1)}), bf16[4,2560,128]{1,2,0:T(8,128)(2,1)}, u32[]{:S(2)}, u32[]{:S(2)}) async-start(bf16[4,2560,128]{1,2,0:T(8,128)(2,1)} %broadcast_in_dim.8), calls=%async_computation | async-start | bytes 5242880 | tf_op jit(solution)/shard_map/all_to_all | solution.py:26
  9.0 0.0 copy-done.3
  9.0 4.1 %collective-permute-start.2 = (bf16[1024,128]{1,0:T(8,128)(2,1)S(1)}, bf16[1024,128]{1,0:T(8,128)(2,1)S(1)}, u32[]{:S(2)}, u32[]{:S(2)}) collective-permute-start(bf16[1024,128]{1,0:T(8,128)(2,1)S(1)} %get-tuple-element.28), channel_id=1, source_target_pairs={{0,4},{4,8},{8,12},{12,16},{16,20},{20,24},{24,28},{28,32},{32,36}... | collective-permute-start | bytes 786440 | tf_op jit(solution)/shard_map/ppermute | solution.py:16
  13.1 5.6 %collective-permute-start.3 = (bf16[1024,128]{1,0:T(8,128)(2,1)S(1)}, bf16[1024,128]{1,0:T(8,128)(2,1)}, u32[]{:S(2)}, u32[]{:S(2)}) collective-permute-start(bf16[1024,128]{1,0:T(8,128)(2,1)S(1)} %get-tuple-element.29), channel_id=1, source_target_pairs={{4,0},{8,4},{12,8},{16,12},{20,16},{24,20},{28,24},{32,28},{36,32}... | collective-permute-start | bytes 786440 | tf_op jit(solution)/shard_map/ppermute | solution.py:19
  18.7 0.0 copy-done.7
  18.7 0.1 copy.40
  18.8 0.1 reshape.48
  18.9 0.0 collective-permute-done.2
  18.9 2.3 %collective-permute-done.3 = bf16[1024,128]{1,0:T(8,128)(2,1)} collective-permute-done((bf16[1024,128]{1,0:T(8,128)(2,1)S(1)}, bf16[1024,128]{1,0:T(8,128)(2,1)}, u32[]{:S(2)}, u32[]{:S(2)}) %collective-permute-start.3) | collective-permute-done | bytes 262176 | tf_op jit(solution)/shard_map/ppermute | solution.py:19
  21.2 1.2 pad_maximum_fusion.1
  22.4 0.0 copy-start.6
  22.4 2.1 %gather_fusion.1 = bf16[60,128,128]{2,1,0:T(8,128)(2,1)} fusion(bf16[36,128,128]{2,1,0:T(8,128)(2,1)S(1)} %bitcast.51, s32[1024]{0:T(1024)S(1)} %pad_clamp_fusion), kind=kCustom, calls=%fused_computation.1 | custom fusion | bytes 3932400 | tf_op jit(solution)/shard_map/gather | solution.py:84
  24.6 10.8 %all-to-all-done = bf16[4,2560,128]{1,2,0:T(8,128)(2,1)} async-done(((bf16[4,2560,128]{1,2,0:T(8,128)(2,1)}), bf16[4,2560,128]{1,2,0:T(8,128)(2,1)}, u32[]{:S(2)}, u32[]{:S(2)}) %all-to-all-start) | async-done | bytes 2621472 | tf_op jit(solution)/shard_map/all_to_all | solution.py:26
  35.4 0.0 copy-done.6
  35.4 3.4 %fusion.5 = (f32[128]{0:T(128)S(1)}, f32[2560,128]{0,1:T(8,128)}) fusion(f32[2560]{0:T(1024)S(1)} %copy-done.6, bf16[2560,512]{0,1:T(8,128)(2,1)} %bitcast.1, bf16[512,512]{1,0:T(8,128)(2,1)} %param.9, s32[]{:T(128)S(6)} %select_n.7), kind=kOutput, calls=%fused_computation.13 | convolution fusion | flops 336527232 | bytes 4073988 | tf_op jit(solution)/shard_map/dot_general | solution.py:115
  38.8 10.2 %all_to_all.27 = f32[2,1,128]{2,1,0:T(1,128)S(1)} all-to-all(f32[2,1,128]{2,1,0:T(1,128)S(1)} %broadcast_in_dim.9), channel_id=1, replica_groups=mesh['rows_0'=16,'rows_1'=4,'rows_2'=2,'cols'=4] {'rows_2'}, dimensions={0} | all-to-all | bytes 2048 | tf_op jit(solution)/shard_map/all_to_all | solution.py:26
  49.1 0.6 broadcast_in_dim.10
  49.7 18.3 %all-to-all-start.2 = ((f32[64,1,128]{2,1,0:T(1,128)}), f32[64,1,128]{2,1,0:T(1,128)S(1)}, u32[]{:S(2)}, u32[]{:S(2)}) async-start(f32[64,1,128]{2,1,0:T(1,128)} %broadcast_in_dim.10), calls=%async_computation.2 | async-start | bytes 65536 | tf_op jit(solution)/shard_map/all_to_all | solution.py:26
  68.0 0.0 copy-done
  68.1 3.1 %fusion.4 = bf16[20,128,128]{1,2,0:T(8,128)(2,1)} fusion(bf16[20,3,128,128]{3,2,1,0:T(8,128)(2,1)S(1)} %copy-done, bf16[20,3,128,128]{3,2,1,0:T(8,128)(2,1)} %bitcast.52), kind=kOutput, calls=%fused_computation.12 | convolution fusion | flops 251985920 | bytes 4587520 | tf_op jit(solution)/shard_map/knij,knjc->kic/dot_general | solution.py:94
  71.1 10.3 %all-to-all-done.2 = f32[64,1,128]{2,1,0:T(1,128)S(1)} async-done(((f32[64,1,128]{2,1,0:T(1,128)}), f32[64,1,128]{2,1,0:T(1,128)S(1)}, u32[]{:S(2)}, u32[]{:S(2)}) %all-to-all-start.2) | async-done | bytes 32800 | tf_op jit(solution)/shard_map/all_to_all | solution.py:26
  81.5 0.0 copy-start.4
  81.5 2.4 %fusion.12 = (bf16[2560,128]{0,1:T(8,128)(2,1)}, f32[2560,128]{0,1:T(8,128)S(1)}) fusion(f32[2560,128]{0,1:T(8,128)} %get-tuple-element.33, f32[128]{0:T(128)S(1)} %rsqrt.7), kind=kLoop, calls=%fused_computation.29 | loop fusion | flops 655360 | bytes 3277312 | tf_op jit(solution)/shard_map/convert_element_type | solution.py:129
  83.9 1.1 fusion.13
  85.0 4.0 %collective-permute-start = (f32[1024,128]{0,1:T(8,128)}, f32[1024,128]{0,1:T(8,128)}, u32[]{:S(2)}, u32[]{:S(2)}) collective-permute-start(f32[1024,128]{0,1:T(8,128)} %get-tuple-element.26), channel_id=1, source_target_pairs={{0,4},{4,8},{8,12},{12,16},{16,20},{20,24},{24,28},{28,32},{32,36}... | collective-permute-start | bytes 1572872 | tf_op jit(solution)/shard_map/ppermute | solution.py:16
  89.0 1.9 %collective-permute-start.1 = (f32[1024,128]{0,1:T(8,128)}, f32[1024,128]{0,1:T(8,128)}, u32[]{:S(2)}, u32[]{:S(2)}) collective-permute-start(f32[1024,128]{0,1:T(8,128)} %get-tuple-element.27), channel_id=1, source_target_pairs={{4,0},{8,4},{12,8},{16,12},{20,16},{24,20},{28,24},{32,28},{36,32}... | collective-permute-start | bytes 1572872 | tf_op jit(solution)/shard_map/ppermute | solution.py:19
  91.0 0.0 copy-done.4
  91.0 2.7 %convolution_bitcast_fusion.4 = f32[512,128]{0,1:T(8,128)S(1)} fusion(bf16[2560,128]{1,0:T(8,128)(2,1)S(1)} %bitcast.53, bf16[2560,512]{0,1:T(8,128)(2,1)} %bitcast.1), kind=kOutput, calls=%fused_computation.17 | convolution fusion | flops 335544320 | bytes 3538944 | tf_op jit(solution)/shard_map/dot_general | solution.py:116
  93.7 0.8 copy.41
  94.6 0.0 copy-start.5
  94.6 3.7 %convolution_bitcast_fusion.3 = f32[512,128]{0,1:T(8,128)} fusion(bf16[2560,512]{0,1:T(8,128)(2,1)} %bitcast.1, bf16[2560,128]{0,1:T(8,128)(2,1)} %copy-done.2, f32[2560]{0:T(1024)S(1)} %copy-done.6), kind=kOutput, calls=%fused_computation.16 | convolution fusion | flops 336527360 | bytes 3549184 | tf_op jit(solution)/shard_map/dot_general | solution.py:119
  98.2 1.8 %copy.43 = f32[512,128]{1,0:T(8,128)} copy(f32[512,128]{0,1:T(8,128)} %convolution_bitcast_fusion.3) | data formatting | bytes 524288 | tf_op jit(solution)/shard_map/dot_general | solution.py:119
  100.0 0.0 copy-done.5
  100.0 1.1 fusion.9
  101.2 4.5 %all_to_all.28 = f32[2,64,4,256]{3,2,1,0:T(4,128)} all-to-all(f32[2,64,4,256]{3,2,1,0:T(4,128)S(1)} %copy.44), channel_id=1, replica_groups=mesh['rows_0'=16,'rows_1'=4,'rows_2'=2,'cols'=4] {'rows_2'}, dimensions={0} | all-to-all | bytes 1048576 | tf_op jit(solution)/shard_map/all_to_all | solution.py:50
  105.7 1.9 %reduce_sum.48 = f32[64,4,256]{2,1,0:T(4,128)} reduce(f32[2,64,4,256]{3,2,1,0:T(4,128)} %all_to_all.28, f32[]{:T(128)} %constant.10.clone.1), dimensions={0}, to_apply=%region_3.0 | reduce | flops 65536 | bytes 786436 | tf_op jit(solution)/shard_map/reduce_sum | solution.py:51
  107.6 7.4 %all-to-all-start.4 = ((f32[64,4,256]{2,1,0:T(4,128)}), f32[64,4,256]{2,1,0:T(4,128)S(1)}, u32[]{:S(2)}, u32[]{:S(2)}) async-start(f32[64,4,256]{2,1,0:T(4,128)} %reduce_sum.48), calls=%async_computation.4 | async-start | bytes 524288 | tf_op jit(solution)/shard_map/all_to_all | solution.py:58
  115.1 2.2 %copy.46 = bf16[2560,128]{1,0:T(8,128)(2,1)} copy(bf16[2560,128]{0,1:T(8,128)(2,1)} %get-tuple-element.24) | data formatting | bytes 1310720
  117.2 0.0 collective-permute-done
  117.2 0.0 collective-permute-done.1
  117.2 2.8 %pad_maximum_fusion = f32[4608,128]{0,1:T(8,128)} fusion(f32[1024,128]{0,1:T(8,128)} %collective-permute-done.1, f32[2560,128]{0,1:T(8,128)S(1)} %get-tuple-element.25, f32[1024,128]{0,1:T(8,128)} %collective-permute-done), kind=kLoop, calls=%fused_computation.4 | loop fusion | flops 1179648 | bytes 4718592 | tf_op jit(solution)/shard_map/concatenate | solution.py:20
  120.0 3.1 %copy.39 = f32[4608,128]{1,0:T(8,128)} copy(f32[4608,128]{0,1:T(8,128)} %pad_maximum_fusion) | data formatting | bytes 4718592 | tf_op jit(solution)/shard_map/concatenate | solution.py:20
  123.1 4.3 %gather_fusion = f32[60,128,128]{2,1,0:T(8,128)} fusion(f32[36,128,128]{2,1,0:T(8,128)} %bitcast.50, s32[1024]{0:T(1024)S(1)} %pad_clamp_fusion), kind=kCustom, calls=%fused_computation | custom fusion | bytes 7864560 | tf_op jit(solution)/shard_map/gather | solution.py:84
  127.4 0.0 copy-start.1
  127.4 4.2 %fusion.1 = f32[20,128,128]{1,2,0:T(8,128)S(1)} fusion(bf16[20,3,128,128]{3,2,1,0:T(8,128)(2,1)S(1)} %copy-done, f32[20,3,128,128]{3,2,1,0:T(8,128)} %bitcast.48), kind=kOutput, calls=%fused_computation.7 | convolution fusion | flops 255590400 | bytes 7208960 | tf_op jit(solution)/shard_map/knij,knjc->kic/dot_general | solution.py:90
  131.6 0.2 copy-done.1
  131.8 1.6 %fusion.3 = bf16[20,128,128]{1,2,0:T(8,128)(2,1)} fusion(f32[20,128,128]{1,2,0:T(8,128)S(1)} %fusion.1, bf16[20,3,128,128]{3,2,1,0:T(8,128)(2,1)S(1)} %copy-done, f32[20,3,128,128]{3,2,1,0:T(8,128)S(1)} %bitcast.49), kind=kOutput, calls=%fused_computation.11 | convolution fusion | flops 253296640 | bytes 7864320 | tf_op jit(solution)/shard_map/knij,knjc->kic/dot_general | solution.py:87
  133.4 1.8 %all-to-all-done.4 = f32[64,4,256]{2,1,0:T(4,128)S(1)} async-done(((f32[64,4,256]{2,1,0:T(4,128)}), f32[64,4,256]{2,1,0:T(4,128)S(1)}, u32[]{:S(2)}, u32[]{:S(2)}) %all-to-all-start.4) | async-done | bytes 262176 | tf_op jit(solution)/shard_map/all_to_all | solution.py:58
  135.3 0.1 reduce_sum.49
  135.3 0.6 fusion.15
  (9 shorter events, 0.1 us)
Async XLA Ops:
  0.6 67.4 %copy-start = (bf16[20,3,128,128]{3,2,1,0:T(8,128)(2,1)S(1)}, bf16[20,3,128,128]{3,2,1,0:T(8,128)(2,1)}, u32[]{:S(2)}) copy-start(bf16[20,3,128,128]{3,2,1,0:T(8,128)(2,1)} %param.6) | copy-start | bytes 5898244
  2.1 1.7 %copy-start.2 = (bf16[2560,128]{0,1:T(8,128)(2,1)}, bf16[2560,128]{0,1:T(8,128)(2,1)S(1)}, u32[]{:S(2)}) copy-start(bf16[2560,128]{0,1:T(8,128)(2,1)S(1)} %copy.36) | copy-start | bytes 1966084
  3.8 5.1 %copy-start.3 = (bf16[2560,128]{1,0:T(8,128)(2,1)S(1)}, bf16[2560,128]{1,0:T(8,128)(2,1)}, u32[]{:S(2)}) copy-start(bf16[2560,128]{1,0:T(8,128)(2,1)} %param.5) | copy-start | bytes 1966084
  3.8 14.8 %copy-start.7 = (s32[20,3]{0,1:T(4,128)S(1)}, s32[20,3]{0,1:T(4,128)}, u32[]{:S(2)}) copy-start(s32[20,3]{0,1:T(4,128)} %param.7) | copy-start | bytes 724
  3.8 31.5 %all-to-all-start = ((bf16[4,2560,128]{1,2,0:T(8,128)(2,1)}), bf16[4,2560,128]{1,2,0:T(8,128)(2,1)}, u32[]{:S(2)}, u32[]{:S(2)}) async-start(bf16[4,2560,128]{1,2,0:T(8,128)(2,1)} %broadcast_in_dim.8), calls=%async_computation | async-start | bytes 5242880 | tf_op jit(solution)/shard_map/all_to_all | solution.py:26
  9.0 9.9 %collective-permute-start.2 = (bf16[1024,128]{1,0:T(8,128)(2,1)S(1)}, bf16[1024,128]{1,0:T(8,128)(2,1)S(1)}, u32[]{:S(2)}, u32[]{:S(2)}) collective-permute-start(bf16[1024,128]{1,0:T(8,128)(2,1)S(1)} %get-tuple-element.28), channel_id=1, source_target_pairs={{0,4},{4,8},{8,12},{12,16},{16,20},{20,24},{24,28},{28,32},{32,36}... | collective-permute-start | bytes 786440 | tf_op jit(solution)/shard_map/ppermute | solution.py:16
  13.1 8.1 %collective-permute-start.3 = (bf16[1024,128]{1,0:T(8,128)(2,1)S(1)}, bf16[1024,128]{1,0:T(8,128)(2,1)}, u32[]{:S(2)}, u32[]{:S(2)}) collective-permute-start(bf16[1024,128]{1,0:T(8,128)(2,1)S(1)} %get-tuple-element.29), channel_id=1, source_target_pairs={{4,0},{8,4},{12,8},{16,12},{20,16},{24,20},{28,24},{32,28},{36,32}... | collective-permute-start | bytes 786440 | tf_op jit(solution)/shard_map/ppermute | solution.py:19
  22.4 13.0 %copy-start.6 = (f32[2560]{0:T(1024)S(1)}, f32[2560]{0:T(1024)}, u32[]{:S(2)}) copy-start(f32[2560]{0:T(1024)} %param.8) | copy-start | bytes 30724
  49.7 31.7 %all-to-all-start.2 = ((f32[64,1,128]{2,1,0:T(1,128)}), f32[64,1,128]{2,1,0:T(1,128)S(1)}, u32[]{:S(2)}, u32[]{:S(2)}) async-start(f32[64,1,128]{2,1,0:T(1,128)} %broadcast_in_dim.10), calls=%async_computation.2 | async-start | bytes 65536 | tf_op jit(solution)/shard_map/all_to_all | solution.py:26
  81.5 9.5 %copy-start.4 = (bf16[20,128,128]{1,2,0:T(8,128)(2,1)S(1)}, bf16[20,128,128]{1,2,0:T(8,128)(2,1)}, u32[]{:S(2)}) copy-start(bf16[20,128,128]{1,2,0:T(8,128)(2,1)} %fusion.4) | copy-start | bytes 1966084
  85.0 32.2 %collective-permute-start = (f32[1024,128]{0,1:T(8,128)}, f32[1024,128]{0,1:T(8,128)}, u32[]{:S(2)}, u32[]{:S(2)}) collective-permute-start(f32[1024,128]{0,1:T(8,128)} %get-tuple-element.26), channel_id=1, source_target_pairs={{0,4},{4,8},{8,12},{12,16},{16,20},{20,24},{24,28},{28,32},{32,36}... | collective-permute-start | bytes 1572872 | tf_op jit(solution)/shard_map/ppermute | solution.py:16
  89.0 28.2 %collective-permute-start.1 = (f32[1024,128]{0,1:T(8,128)}, f32[1024,128]{0,1:T(8,128)}, u32[]{:S(2)}, u32[]{:S(2)}) collective-permute-start(f32[1024,128]{0,1:T(8,128)} %get-tuple-element.27), channel_id=1, source_target_pairs={{4,0},{8,4},{12,8},{16,12},{20,16},{24,20},{28,24},{32,28},{36,32}... | collective-permute-start | bytes 1572872 | tf_op jit(solution)/shard_map/ppermute | solution.py:19
  94.6 5.5 %copy-start.5 = (f32[512,128]{1,0:T(8,128)S(1)}, f32[512,128]{1,0:T(8,128)}, u32[]{:S(2)}) copy-start(f32[512,128]{1,0:T(8,128)} %copy.41) | copy-start | bytes 786436
  107.6 27.6 %all-to-all-start.4 = ((f32[64,4,256]{2,1,0:T(4,128)}), f32[64,4,256]{2,1,0:T(4,128)S(1)}, u32[]{:S(2)}, u32[]{:S(2)}) async-start(f32[64,4,256]{2,1,0:T(4,128)} %reduce_sum.48), calls=%async_computation.4 | async-start | bytes 524288 | tf_op jit(solution)/shard_map/all_to_all | solution.py:58
  127.4 4.4 %copy-start.1 = (f32[60,128,128]{2,1,0:T(8,128)S(1)}, f32[60,128,128]{2,1,0:T(8,128)}, u32[]{:S(2)}) copy-start(f32[60,128,128]{2,1,0:T(8,128)} %gather_fusion) | copy-start | bytes 11796484
where the time goes:
time: 138 us; the launch traced here: 136 us
  starting transfers between devices  46.4 us (34%)
  waiting for transfers between devices  25.3 us (18%)
  local copies, waits for them, and re-layouts  20.3 us (15%)
  matrix products  18.7 us (14%)
  blocking collectives  14.8 us (11%)
  other arithmetic  9.64 us (7%)
    all_to_all x2, starting transfers between devices, from_everyone(): lax.all_to_all(jnp.broadcast_to(value[None], (size, *value.shape)), axis,...  23.4 us
    all_to_all x2, waiting for transfers between devices, from_everyone(): lax.all_to_all(jnp.broadcast_to(value[None], (size, *value.shape)), axis,...  21.1 us
    all_to_all x1, blocking collectives, from_everyone(): lax.all_to_all(jnp.broadcast_to(value[None], (size, *value.shape)), axis,...  10.2 us
    ppermute x2, starting transfers between devices, with_halo(): lax.ppermute(lax.slice_in_dim(block, block.shape[dim] - width, None, axis...  8.1 us
    ppermute x2, starting transfers between devices, with_halo(): lax.ppermute(lax.slice_in_dim(block, 0, width, axis=dim), axis, backward)  7.48 us
    all_to_all x1, starting transfers between devices, summed_rows(): lax.all_to_all(nearer, far, split_axis=0, concat_axis=0, tiled=True)  7.42 us
    gather x2, local copies, waits for them, and re-layouts, apply_blocks(): source = tiles[local_index]  6.46 us
    all_to_all x1, blocking collectives, sent_and_summed(): tiles = lax.all_to_all(cut_along(value, dim, size), axis, 0, 0, tiled=True)  4.53 us
  transfers between devices with their start and end apart: 7, of which 4 were waited for; matrix products, arithmetic and copies ran while one was open for 27% of the time, Pallas kernels for 0%

commit v1 on v0

v1 whole, which is shorter than its diff:
```python
import jax
import jax.numpy as jnp
from jax import lax
from jax.sharding import Mesh
from jax.sharding import PartitionSpec as P

BAND = 8
ROWS = ("rows_0", "rows_1", "rows_2")


def with_halo(block, sides, width):
    for axis, dim in sides:
        count = lax.axis_size(axis)
        forward = [(i, i + 1) for i in range(count - 1)]
        backward = [(target, source) for source, target in forward]
        low = lax.ppermute(
            lax.slice_in_dim(block, block.shape[dim] - width, None, axis=dim), axis, forward
        )
        high = lax.ppermute(lax.slice_in_dim(block, 0, width, axis=dim), axis, backward)
        block = jnp.concatenate([low, block, high], axis=dim)
    return block


def from_everyone(value, axis):
    size = lax.axis_size(axis)
    return lax.all_to_all(
        jnp.broadcast_to(value[None], (size, *value.shape)), axis, 0, 0, tiled=True
    )


def laid_out(tiles, dim):
    shape = list(tiles.shape[1:])
    shape[dim] *= tiles.shape[0]
    return jnp.moveaxis(tiles, 0, dim).reshape(shape)


def gather_directly(value, axis, dim):
    tiles = from_everyone(value, axis)
    return laid_out(tiles, dim)


def cut_along(value, dim, size):
    shape = value.shape
    tiles = value.reshape(*shape[:dim], size, shape[dim] // size, *shape[dim + 1 :])
    return jnp.moveaxis(tiles, dim, 0)


def sent_and_summed(value, axis, dim):
    size = lax.axis_size(axis)
    tiles = lax.all_to_all(cut_along(value, dim, size), axis, 0, 0, tiled=True)
    return jnp.sum(tiles, axis=0)


def apply_blocks(padded, stiff_blocks, block_neighbors, first_block):
    block_count = stiff_blocks.shape[0]
    block_size = stiff_blocks.shape[2]
    col_width = padded.shape[1]
    tiles = padded.reshape(block_count + 2 * BAND, block_size, col_width)
    local_index = block_neighbors - first_block + BAND
    source = tiles[local_index]
    result = jnp.einsum(
        "knij,knjc->kic", stiff_blocks, source, preferred_element_type=jnp.float32
    )
    return result.reshape(block_count * block_size, col_width)


def body(basis_rows, stiff_blocks, block_neighbors, vertex_mass, rotation):
    row_count = lax.axis_size(ROWS)
    row_place = lax.axis_index(ROWS)
    col_place = lax.axis_index("cols")
    local_rows, col_width = basis_rows.shape
    block_count = stiff_blocks.shape[0]
    block_size = stiff_blocks.shape[2]
    vertices = local_rows * row_count
    first_block = row_place * block_count
    near, far = "rows_2", ("rows_0", "rows_1")
    local_turn = lax.dynamic_slice_in_dim(rotation, col_place * col_width, col_width, 1)
    padded = with_halo(basis_rows, ((ROWS, 0),), BAND * block_size)
    piece = gather_directly(basis_rows, "cols", 1)
    stiff_rows = apply_blocks(padded, stiff_blocks, block_neighbors, first_block)
    half_image = stiff_rows.astype(jnp.bfloat16)
    weighted = (vertex_mass[:, None] * basis_rows.astype(jnp.float32)).astype(jnp.bfloat16)
    turned = jnp.dot(piece, local_turn, preferred_element_type=jnp.float32)
    turned_half = turned.astype(jnp.bfloat16)
    rimmed = with_halo(turned_half, ((ROWS, 0),), BAND * block_size)
    stiff_part = lax.dot_general(
        piece, half_image, (((0,), (0,)), ((), ())), preferred_element_type=jnp.float32
    )
    mass_part = lax.dot_general(
        piece, weighted, (((0,), (0,)), ((), ())), preferred_element_type=jnp.float32
    )
    squares = jnp.sum(vertex_mass[:, None] * turned * turned, axis=0)
    parts = jnp.concatenate([stiff_part, mass_part], axis=1)
    wide = jnp.zeros((2 * col_width,), jnp.float32).at[:col_width].set(squares)
    tiles = cut_along(parts, 0, lax.axis_size(far))
    nearer = sent_and_summed(
        jnp.concatenate(
            [
                tiles.reshape(lax.axis_size(far), 2, -1, 2 * col_width),
                jnp.broadcast_to(wide, (lax.axis_size(far), 2, 1, 2 * col_width)),
            ],
            axis=2,
        ).reshape(lax.axis_size(far), -1, 2 * col_width),
        near,
        1,
    )
    arrived = lax.all_to_all(nearer, far, split_axis=0, concat_axis=0, tiled=True)
    grams = arrived.sum(axis=0) / vertices
    product = apply_blocks(rimmed, stiff_blocks, block_neighbors, first_block)
    scale = lax.rsqrt(grams[-1, :col_width])
    new_basis = (turned * scale).astype(jnp.bfloat16)
    stiff_image = (product * scale).astype(jnp.bfloat16)
    return (new_basis, stiff_image, grams[:-1, :col_width], grams[:-1, col_width:])


def solution(mesh):
    split = Mesh(
        mesh.devices.reshape(16, 4, 2, mesh.shape["cols"]), ("rows_0", "rows_1", "rows_2", "cols")
    )
    in_specs = (P(ROWS, "cols"), P(ROWS, None, None, None), P(ROWS, None), P(ROWS), P())
    out_specs = (P(ROWS, "cols"), P(ROWS, "cols"), P(ROWS, "cols"), P(ROWS, "cols"))
    return jax.shard_map(body, mesh=split, in_specs=in_specs, out_specs=out_specs, check_vma=False)
```

time: 138 us -> 139 us (level)
  blocking collectives: 14.8 us -> 60.8 us
  starting transfers between devices: 46.4 us -> 22.4 us
  waiting for transfers between devices: 25.3 us -> 13.8 us
  matrix products: 18.7 us -> 12.5 us
  local copies, waits for them, and re-layouts: 20.3 us -> 18.4 us
    all_to_all x1, blocking collectives: 10.2 us -> 49.2 us  [body(): lax.all_to_all(nearer, far, split_axis=0, concat_axis=0, tiled=True)]
    all_to_all x2 -> x1, starting transfers between devices: 23.4 us -> 5.13 us  [from_everyone(): lax.all_to_all(jnp.broadcast_to(value[None], (size, *value.shape)), axis,...]
    all_to_all x2 -> x1, waiting for transfers between devices: 21.1 us -> 8.49 us  [from_everyone(): lax.all_to_all(jnp.broadcast_to(value[None], (size, *value.shape)), axis,...]
    all_to_all x1 -> x0, starting transfers between devices: 7.42 us -> none  [summed_rows(): lax.all_to_all(nearer, far, split_axis=0, concat_axis=0, tiled=True)]
    all_to_all x1, blocking collectives: 4.53 us -> 11.6 us  [sent_and_summed(): tiles = lax.all_to_all(cut_along(value, dim, size), axis, 0, 0, tiled=True)]
    dot_general x3 -> x1, matrix products: 9.19 us -> 2.5 us  [body(): turned = jnp.dot(piece, local_turn, preferred_element_type=jnp.float32)]
    ppermute x2, waiting for transfers between devices: 2.28 us -> 5.29 us  [with_halo(): lax.ppermute(lax.slice_in_dim(block, 0, width, axis=dim), axis, backward)]
    dot_general x2 -> x0, local copies, waits for them, and re-layouts: 2.61 us -> none  [the longest x1 1.78 us: body(): lax.dot_general(piece, weighted, (((0,), (0,)), ((), ())), preferred_elem...]
  transfers between devices with their start and end apart: 7 -> 5, of which waited for: 4 -> 3; matrix products, arithmetic and copies ran while one was open for 27% -> 6% of each run, Pallas kernels for 0% -> 0%
where the time goes in v1:
time: 139 us; the launch traced here: 138 us
  blocking collectives  60.8 us (44%)
  starting transfers between devices  22.4 us (16%)
  local copies, waits for them, and re-layouts  18.4 us (13%)
  waiting for transfers between devices  13.8 us (10%)
  matrix products  12.5 us (9%)
  other arithmetic  9.13 us (7%)
    all_to_all x1, blocking collectives, body(): lax.all_to_all(nearer, far, split_axis=0, concat_axis=0, tiled=True)  49.2 us
    all_to_all x1, blocking collectives, sent_and_summed(): tiles = lax.all_to_all(cut_along(value, dim, size), axis, 0, 0, tiled=True)  11.6 us
    ppermute x2, starting transfers between devices, with_halo(): lax.ppermute(lax.slice_in_dim(block, block.shape[dim] - width, None, axis...  9.81 us
    all_to_all x1, waiting for transfers between devices, from_everyone(): lax.all_to_all(jnp.broadcast_to(value[None], (size, *value.shape)), axis,...  8.49 us
    ppermute x2, starting transfers between devices, with_halo(): lax.ppermute(lax.slice_in_dim(block, 0, width, axis=dim), axis, backward)  7.48 us
    unnamed x19, local copies, waits for them, and re-layouts  5.63 us
    ppermute x2, waiting for transfers between devices, with_halo(): lax.ppermute(lax.slice_in_dim(block, 0, width, axis=dim), axis, backward)  5.29 us
    all_to_all x1, starting transfers between devices, from_everyone(): lax.all_to_all(jnp.broadcast_to(value[None], (size, *value.shape)), axis,...  5.13 us
  transfers between devices with their start and end apart: 5, of which 3 were waited for; matrix products, arithmetic and copies ran while one was open for 6% of the time, Pallas kernels for 0%

profile of v1, /device:TPU:1, one launch (start us, length us, event | category | flops | bytes accessed | tf_op | source)
XLA Modules:
  0.0 137.9 jit_solution(17499521085768661359)
XLA Ops:
  0.6 0.0 copy-start
  0.6 1.5 %copy.41 = bf16[2560,128]{0,1:T(8,128)(2,1)S(1)} copy(bf16[2560,128]{1,0:T(8,128)(2,1)} %param.7) | data formatting | bytes 1310720 | tf_op args[0]
  2.1 0.0 copy-start.1
  2.1 1.7 %broadcast_in_dim.6 = bf16[4,2560,128]{1,2,0:T(8,128)(2,1)} broadcast(bf16[2560,128]{0,1:T(8,128)(2,1)S(1)} %copy.41), dimensions={1,2} | broadcast | bytes 3276800 | tf_op jit(solution)/shard_map/broadcast_in_dim | solution.py:27
  3.8 0.0 copy-start.3
  3.9 0.0 copy-start.7
  3.9 0.0 copy-done.1
  3.9 5.1 %all-to-all-start = ((bf16[4,2560,128]{1,2,0:T(8,128)(2,1)}), bf16[4,2560,128]{1,2,0:T(8,128)(2,1)}, u32[]{:S(2)}, u32[]{:S(2)}) async-start(bf16[4,2560,128]{1,2,0:T(8,128)(2,1)} %broadcast_in_dim.6), calls=%async_computation | async-start | bytes 5242880 | tf_op jit(solution)/shard_map/all_to_all | solution.py:26
  9.0 0.0 copy-done.3
  9.0 4.1 %collective-permute-start = (bf16[1024,128]{1,0:T(8,128)(2,1)S(1)}, bf16[1024,128]{1,0:T(8,128)(2,1)S(1)}, u32[]{:S(2)}, u32[]{:S(2)}) collective-permute-start(bf16[1024,128]{1,0:T(8,128)(2,1)S(1)} %get-tuple-element.40), channel_id=1, source_target_pairs={{0,4},{4,8},{8,12},{12,16},{16,20},{20,24},{24,28},{28,32},{32,36}... | collective-permute-start | bytes 786440 | tf_op jit(solution)/shard_map/ppermute | solution.py:16
  13.1 5.6 %collective-permute-start.1 = (bf16[1024,128]{1,0:T(8,128)(2,1)S(1)}, bf16[1024,128]{1,0:T(8,128)(2,1)}, u32[]{:S(2)}, u32[]{:S(2)}) collective-permute-start(bf16[1024,128]{1,0:T(8,128)(2,1)S(1)} %get-tuple-element.41), channel_id=1, source_target_pairs={{4,0},{8,4},{12,8},{16,12},{20,16},{24,20},{28,24},{32,28},{36,32}... | collective-permute-start | bytes 786440 | tf_op jit(solution)/shard_map/ppermute | solution.py:19
  18.7 0.0 copy-done.7
  18.7 0.1 copy.42
  18.8 0.1 reshape.52
  18.9 0.0 collective-permute-done
  18.9 2.3 %collective-permute-done.1 = bf16[1024,128]{1,0:T(8,128)(2,1)} collective-permute-done((bf16[1024,128]{1,0:T(8,128)(2,1)S(1)}, bf16[1024,128]{1,0:T(8,128)(2,1)}, u32[]{:S(2)}, u32[]{:S(2)}) %collective-permute-start.1) | collective-permute-done | bytes 262176 | tf_op jit(solution)/shard_map/ppermute | solution.py:19
  21.2 1.2 pad_maximum_fusion
  22.5 2.1 %gather_fusion = bf16[60,128,128]{2,1,0:T(8,128)(2,1)} fusion(bf16[36,128,128]{2,1,0:T(8,128)(2,1)S(1)} %bitcast.39, s32[1024]{0:T(1024)S(1)} %pad_clamp_fusion), kind=kCustom, calls=%fused_computation | custom fusion | bytes 3932400 | tf_op jit(solution)/shard_map/gather | solution.py:60
  24.6 0.0 copy-done
  24.6 0.0 copy-start.2
  24.6 0.0 copy-start.6
  24.6 2.3 %fusion = bf16[20,128,128]{1,2,0:T(8,128)(2,1)S(1)} fusion(bf16[20,3,128,128]{3,2,1,0:T(8,128)(2,1)S(1)} %copy-done, bf16[20,3,128,128]{3,2,1,0:T(8,128)(2,1)} %bitcast.42), kind=kOutput, calls=%fused_computation.5 | convolution fusion | flops 251985920 | bytes 4587520 | tf_op jit(solution)/shard_map/knij,knjc->kic/dot_general | solution.py:61
  26.9 8.5 %all-to-all-done = bf16[4,2560,128]{1,2,0:T(8,128)(2,1)} async-done(((bf16[4,2560,128]{1,2,0:T(8,128)(2,1)}), bf16[4,2560,128]{1,2,0:T(8,128)(2,1)}, u32[]{:S(2)}, u32[]{:S(2)}) %all-to-all-start) | async-done | bytes 2621472 | tf_op jit(solution)/shard_map/all_to_all | solution.py:26
  35.4 0.0 copy-done.2
  35.4 0.0 copy-done.6
  35.4 2.7 %convolution_bitcast_fusion.2 = f32[512,128]{0,1:T(8,128)S(1)} fusion(bf16[2560,512]{0,1:T(8,128)(2,1)} %bitcast.1, bf16[2560,128]{0,1:T(8,128)(2,1)S(1)} %copy-done.2, f32[2560]{0:T(1024)S(1)} %copy-done.6), kind=kOutput, calls=%fused_computation.12 | convolution fusion | flops 336527360 | bytes 3549184 | tf_op jit(solution)/shard_map/dot_general | solution.py:89
  38.1 2.7 %convolution_bitcast_fusion.3 = f32[512,128]{0,1:T(8,128)S(1)} fusion(bf16[2560,128]{1,0:T(8,128)(2,1)S(1)} %bitcast.44, bf16[2560,512]{0,1:T(8,128)(2,1)} %bitcast.1), kind=kOutput, calls=%fused_computation.13 | convolution fusion | flops 335544320 | bytes 3538944 | tf_op jit(solution)/shard_map/dot_general | solution.py:86
  40.9 0.2 copy.44
  41.1 0.9 reshape_reshape.3
  42.0 0.0 copy-start.5
  42.0 2.5 %fusion.1 = (f32[128]{0:T(128)S(1)}, f32[2560,128]{0,1:T(8,128)S(1)}) fusion(f32[2560]{0:T(1024)S(1)} %copy-done.6, bf16[2560,512]{0,1:T(8,128)(2,1)} %bitcast.1, bf16[512,512]{1,0:T(8,128)(2,1)} %param.11, s32[]{:T(128)S(6)} %select_n.7), kind=kOutput, calls=%fused_computation.6 | convolution fusion | flops 336527232 | bytes 4073988 | tf_op jit(solution)/shard_map/dot_general | solution.py:83
  44.5 0.1 broadcast_in_dim.8
  44.6 0.0 copy-done.5
  44.6 0.2 maximum_bitcast_fusion
  44.9 0.4 copy.45
  45.2 11.6 %all_to_all.15 = f32[2,64,5,256]{3,1,2,0:T(8,128)} all-to-all(f32[2,64,5,256]{3,1,2,0:T(8,128)S(1)} %copy.45), channel_id=1, replica_groups=mesh['rows_0'=16,'rows_1'=4,'rows_2'=2,'cols'=4] {'rows_2'}, dimensions={0} | all-to-all | bytes 1310720 | tf_op jit(solution)/shard_map/all_to_all | solution.py:50
  56.8 1.9 %reduce_sum.28 = f32[64,5,256]{2,0,1:T(8,128)} reduce(f32[2,64,5,256]{3,1,2,0:T(8,128)} %all_to_all.15, f32[]{:T(128)} %constant.62.clone.1), dimensions={0}, to_apply=%region_1.0 | reduce | flops 81920 | bytes 983044 | tf_op jit(solution)/shard_map/reduce_sum | solution.py:51
  58.7 1.2 copy.46
  59.9 49.2 %all_to_all.16 = f32[64,5,256]{2,1,0:T(8,128)} all-to-all(f32[64,5,256]{2,1,0:T(8,128)S(1)} %copy.46), channel_id=1, replica_groups=mesh['rows_0'=16,'rows_1'=4,'rows_2'=2,'cols'=4] {'rows_0','rows_1'}, dimensions={0} | all-to-all | bytes 655360 | tf_op jit(solution)/shard_map/all_to_all | solution.py:107
  109.1 1.1 reduce_sum.29
  110.2 1.0 fusion.6
  111.2 0.0 copy-start.4
  111.2 0.9 copy-done.4
  112.2 5.7 %collective-permute-start.2 = (bf16[1024,128]{0,1:T(8,128)(2,1)S(1)}, bf16[1024,128]{0,1:T(8,128)(2,1)S(1)}, u32[]{:S(2)}, u32[]{:S(2)}) collective-permute-start(bf16[1024,128]{0,1:T(8,128)(2,1)S(1)} %get-tuple-element.38), channel_id=1, source_target_pairs={{0,4},{4,8},{8,12},{12,16},{16,20},{20,24},{24,28},{28,32},{32,36}... | collective-permute-start | bytes 786440 | tf_op jit(solution)/shard_map/ppermute | solution.py:16
  117.9 1.9 %collective-permute-start.3 = (bf16[1024,128]{0,1:T(8,128)(2,1)S(1)}, bf16[1024,128]{0,1:T(8,128)(2,1)S(1)}, u32[]{:S(2)}, u32[]{:S(2)}) collective-permute-start(bf16[1024,128]{0,1:T(8,128)(2,1)S(1)} %get-tuple-element.39), channel_id=1, source_target_pairs={{4,0},{8,4},{12,8},{16,12},{20,16},{24,20},{28,24},{32,28},{36,32}... | collective-permute-start | bytes 786440 | tf_op jit(solution)/shard_map/ppermute | solution.py:19
  119.8 2.2 %copy.49 = bf16[2560,128]{1,0:T(8,128)(2,1)} copy(bf16[2560,128]{0,1:T(8,128)(2,1)} %get-tuple-element.37) | data formatting | bytes 1310720
  122.0 0.6 fusion.9
  122.6 0.0 collective-permute-done.2
  122.6 3.0 %collective-permute-done.3 = bf16[1024,128]{0,1:T(8,128)(2,1)S(1)} collective-permute-done((bf16[1024,128]{0,1:T(8,128)(2,1)S(1)}, bf16[1024,128]{0,1:T(8,128)(2,1)S(1)}, u32[]{:S(2)}, u32[]{:S(2)}) %collective-permute-start.3) | collective-permute-done | bytes 262176 | tf_op jit(solution)/shard_map/ppermute | solution.py:19
  125.6 2.2 %pad_maximum_fusion.1 = bf16[4608,128]{0,1:T(8,128)(2,1)} fusion(bf16[1024,128]{0,1:T(8,128)(2,1)S(1)} %collective-permute-done.3, bf16[2560,128]{0,1:T(8,128)(2,1)} %copy-done.4, bf16[1024,128]{0,1:T(8,128)(2,1)S(1)} %collective-permute-done.2), kind=kLoop, calls=%fused_computation.11 | loop fusion | flops 3538944 | bytes 2359296 | tf_op jit(solution)/shard_map/concatenate | solution.py:20
  127.8 1.7 %copy.47 = bf16[4608,128]{1,0:T(8,128)(2,1)S(1)} copy(bf16[4608,128]{0,1:T(8,128)(2,1)} %pad_maximum_fusion.1) | data formatting | bytes 2359296 | tf_op jit(solution)/shard_map/concatenate | solution.py:20
  129.5 2.1 %gather_fusion.1 = bf16[60,128,128]{2,1,0:T(8,128)(2,1)} fusion(bf16[36,128,128]{2,1,0:T(8,128)(2,1)S(1)} %bitcast.40, s32[1024]{0:T(1024)S(1)} %pad_clamp_fusion), kind=kCustom, calls=%fused_computation.1 | custom fusion | bytes 3932400 | tf_op jit(solution)/shard_map/gather | solution.py:60
  131.6 2.2 %fusion.10 = f32[20,128,128,1]{1,2,3,0:T(8,128)S(1)} fusion(bf16[20,3,128,128]{3,2,1,0:T(8,128)(2,1)S(1)} %copy-done, bf16[20,3,128,128]{3,2,1,0:T(8,128)(2,1)} %bitcast.41), kind=kOutput, calls=%fused_computation.28 | convolution fusion | flops 251658240 | bytes 5242880 | tf_op jit(solution)/shard_map/knij,knjc->kic/dot_general | solution.py:61
  133.8 1.5 %copy.48 = f32[2560,128]{0,1:T(8,128)} copy(f32[2560,128]{1,0:T(8,128)S(1)} %bitcast.43) | data formatting | bytes 2621440 | tf_op jit(solution)/shard_map/reshape | solution.py:64
  135.3 1.4 %multiply_convert_fusion = bf16[2560,128]{0,1:T(8,128)(2,1)S(1)} fusion(f32[2560,128]{0,1:T(8,128)} %copy.48, f32[128]{0:T(128)S(1)} %fusion.4), kind=kLoop, calls=%fused_computation.7 | loop fusion | flops 655360 | bytes 1966592 | tf_op jit(solution)/shard_map/convert_element_type | solution.py:112
  136.8 1.1 copy.50
  (8 shorter events, 0.1 us)
Async XLA Ops:
  0.6 24.0 %copy-start = (bf16[20,3,128,128]{3,2,1,0:T(8,128)(2,1)S(1)}, bf16[20,3,128,128]{3,2,1,0:T(8,128)(2,1)}, u32[]{:S(2)}) copy-start(bf16[20,3,128,128]{3,2,1,0:T(8,128)(2,1)} %param.8) | copy-start | bytes 5898244
  2.1 1.7 %copy-start.1 = (bf16[2560,128]{0,1:T(8,128)(2,1)}, bf16[2560,128]{0,1:T(8,128)(2,1)S(1)}, u32[]{:S(2)}) copy-start(bf16[2560,128]{0,1:T(8,128)(2,1)S(1)} %copy.41) | copy-start | bytes 1966084
  3.8 5.1 %copy-start.3 = (bf16[2560,128]{1,0:T(8,128)(2,1)S(1)}, bf16[2560,128]{1,0:T(8,128)(2,1)}, u32[]{:S(2)}) copy-start(bf16[2560,128]{1,0:T(8,128)(2,1)} %param.7) | copy-start | bytes 1966084
  3.9 14.8 %copy-start.7 = (s32[20,3]{0,1:T(4,128)S(1)}, s32[20,3]{0,1:T(4,128)}, u32[]{:S(2)}) copy-start(s32[20,3]{0,1:T(4,128)} %param.9) | copy-start | bytes 724
  3.9 31.5 %all-to-all-start = ((bf16[4,2560,128]{1,2,0:T(8,128)(2,1)}), bf16[4,2560,128]{1,2,0:T(8,128)(2,1)}, u32[]{:S(2)}, u32[]{:S(2)}) async-start(bf16[4,2560,128]{1,2,0:T(8,128)(2,1)} %broadcast_in_dim.6), calls=%async_computation | async-start | bytes 5242880 | tf_op jit(solution)/shard_map/all_to_all | solution.py:26
  9.0 9.9 %collective-permute-start = (bf16[1024,128]{1,0:T(8,128)(2,1)S(1)}, bf16[1024,128]{1,0:T(8,128)(2,1)S(1)}, u32[]{:S(2)}, u32[]{:S(2)}) collective-permute-start(bf16[1024,128]{1,0:T(8,128)(2,1)S(1)} %get-tuple-element.40), channel_id=1, source_target_pairs={{0,4},{4,8},{8,12},{12,16},{16,20},{20,24},{24,28},{28,32},{32,36}... | collective-permute-start | bytes 786440 | tf_op jit(solution)/shard_map/ppermute | solution.py:16
  13.1 8.1 %collective-permute-start.1 = (bf16[1024,128]{1,0:T(8,128)(2,1)S(1)}, bf16[1024,128]{1,0:T(8,128)(2,1)}, u32[]{:S(2)}, u32[]{:S(2)}) collective-permute-start(bf16[1024,128]{1,0:T(8,128)(2,1)S(1)} %get-tuple-element.41), channel_id=1, source_target_pairs={{4,0},{8,4},{12,8},{16,12},{20,16},{24,20},{28,24},{32,28},{36,32}... | collective-permute-start | bytes 786440 | tf_op jit(solution)/shard_map/ppermute | solution.py:19
  24.6 10.8 %copy-start.2 = (bf16[2560,128]{0,1:T(8,128)(2,1)S(1)}, bf16[2560,128]{0,1:T(8,128)(2,1)}, u32[]{:S(2)}) copy-start(bf16[2560,128]{0,1:T(8,128)(2,1)} %copy-done.1) | copy-start | bytes 1966084
  24.6 10.8 %copy-start.6 = (f32[2560]{0:T(1024)S(1)}, f32[2560]{0:T(1024)}, u32[]{:S(2)}) copy-start(f32[2560]{0:T(1024)} %param.10) | copy-start | bytes 30724
  42.0 2.6 %copy-start.5 = (f32[64,2,4,256]{3,2,1,0:T(4,128)S(1)}, f32[64,2,4,256]{3,2,1,0:T(4,128)}, u32[]{:S(2)}) copy-start(f32[64,2,4,256]{3,2,1,0:T(4,128)} %reshape_reshape.3) | copy-start | bytes 1572868
  111.2 0.9 copy-start.4
  112.2 10.4 %collective-permute-start.2 = (bf16[1024,128]{0,1:T(8,128)(2,1)S(1)}, bf16[1024,128]{0,1:T(8,128)(2,1)S(1)}, u32[]{:S(2)}, u32[]{:S(2)}) collective-permute-start(bf16[1024,128]{0,1:T(8,128)(2,1)S(1)} %get-tuple-element.38), channel_id=1, source_target_pairs={{0,4},{4,8},{8,12},{12,16},{16,20},{20,24},{24,28},{28,32},{32,36}... | collective-permute-start | bytes 786440 | tf_op jit(solution)/shard_map/ppermute | solution.py:16
  117.9 7.7 %collective-permute-start.3 = (bf16[1024,128]{0,1:T(8,128)(2,1)S(1)}, bf16[1024,128]{0,1:T(8,128)(2,1)S(1)}, u32[]{:S(2)}, u32[]{:S(2)}) collective-permute-start(bf16[1024,128]{0,1:T(8,128)(2,1)S(1)} %get-tuple-element.39), channel_id=1, source_target_pairs={{4,0},{8,4},{12,8},{16,12},{20,16},{24,20},{28,24},{32,28},{36,32}... | collective-permute-start | bytes 786440 | tf_op jit(solution)/shard_map/ppermute | solution.py:19

commit v2 on v1

v2 whole, which is shorter than its diff:
```python
import functools

import jax
import jax.numpy as jnp
from jax import lax
from jax.experimental import pallas as pl
from jax.experimental.pallas import tpu as pltpu
from jax.sharding import Mesh
from jax.sharding import PartitionSpec as P

BAND = 8
ROWS = ("rows_0", "rows_1", "rows_2")
MESH = pl.DeviceIdType.MESH
F32 = jnp.float32
BF16 = jnp.bfloat16
OWN, LEFT, RIGHT, FAR = 0, 1, 2, 3


def transposed_dot(left, right):
    return lax.dot_general(left, right, (((0,), (0,)), ((), ())), preferred_element_type=F32)


def kernel(
    sizes,
    nb_ref,
    basis_ref,
    blocks_ref,
    mass_ref,
    rot_ref,
    basis_out,
    image_out,
    stiff_out,
    mass_out,
    padded,
    others,
    rimmed,
    turned,
    product,
    mass_col,
    weights,
    blocks,
    turn,
    gram,
    gram_core,
    gram_x,
    gram_x_in,
    gram_z,
    gram_z_in,
    tile_mine,
    tile_in,
    sq_own,
    sq_core,
    sq_x,
    sq_x_in,
    sq_z,
    sq_z_in,
    load_sem,
    y_send,
    y_recv,
    halo_send,
    halo_recv,
    core_send,
    core_recv,
    x_send,
    x_recv,
    z_send,
    z_recv,
):
    nz, nx, ny, count, size, width, parts = sizes
    z, x, k = (lax.axis_index(a) for a in ROWS)
    y = lax.axis_index("cols")
    rows = count * size
    half = count // 2
    piece = half // parts
    vertices = rows * nz * nx * 2
    place = (z * nx + x) * 2 + k
    total = nz * nx * 2

    def row_device(index):
        index = lax.rem(index + total, total)
        return {
            "rows_0": lax.div(index, 2 * nx),
            "rows_1": lax.rem(lax.div(index, 2), nx),
            "rows_2": lax.rem(index, 2),
        }

    up, down = row_device(place + 1), row_device(place - 1)
    y_right, y_left = {"cols": lax.rem(y + 1, ny)}, {"cols": lax.rem(y + ny - 1, ny)}
    partner = {"rows_2": 1 - k}
    x_peers = [{"rows_1": lax.rem(x + d, nx)} for d in range(1, nx)]
    z_peers = [{"rows_0": lax.rem(z + d, nz)} for d in range(1, nz)]
    col_of = [y, lax.rem(y + ny - 1, ny), lax.rem(y + 1, ny), lax.rem(y + 2, ny)]

    load_basis = pltpu.make_async_copy(basis_ref, padded.at[pl.ds(BAND, count)], load_sem.at[0])
    load_basis.start()
    load_turn = []
    for i in range(ny):
        load = pltpu.make_async_copy(
            rot_ref.at[
                pl.ds(pl.multiple_of(col_of[i] * width, width), width),
                pl.ds(pl.multiple_of(y * width, width), width),
            ],
            turn.at[pl.ds(i * width, width)],
            load_sem.at[2 + i],
        )
        load.start()
        load_turn.append(load)
    load_blocks = pltpu.make_async_copy(blocks_ref, blocks, load_sem.at[1])
    load_blocks.start()

    peers = [up, down, y_right, y_left, partner, *x_peers, *z_peers]
    barrier = pltpu.get_barrier_semaphore()
    for peer in peers:
        pl.semaphore_signal(barrier, inc=1, device_id=peer, device_id_type=MESH)
    pl.semaphore_wait(barrier, len(peers))

    started = []

    def send(source, target, send_sem, recv_sem, device):
        copy = pltpu.make_async_remote_copy(
            src_ref=source,
            dst_ref=target,
            send_sem=send_sem,
            recv_sem=recv_sem,
            device_id=device,
            device_id_type=MESH,
        )
        copy.start()
        started.append(copy)
        return copy

    load_basis.wait()
    low, high = pl.ds(0, half), pl.ds(half, half)
    mine_low, mine_high = pl.ds(BAND, half), pl.ds(BAND + half, half)
    left_first = send(
        padded.at[mine_low], others.at[0, low], y_send.at[0], y_recv.at[0], y_right
    )
    right_first = send(
        padded.at[mine_high], others.at[1, high], y_send.at[1], y_recv.at[1], y_left
    )
    first_rows, last_rows = pl.ds(BAND, BAND), pl.ds(count, BAND)
    before, after = pl.ds(0, BAND), pl.ds(BAND + count, BAND)
    halo_low = send(
        padded.at[last_rows], padded.at[before], halo_send.at[0], halo_recv.at[0], up
    )
    halo_high = send(
        padded.at[first_rows], padded.at[after], halo_send.at[1], halo_recv.at[1], down
    )
    left_second = send(
        padded.at[mine_high], others.at[0, high], y_send.at[2], y_recv.at[2], y_right
    )
    right_second = send(
        padded.at[mine_low], others.at[1, low], y_send.at[3], y_recv.at[3], y_left
    )

    for b in range(count):
        at = pl.ds(b * size, size)
        column = jnp.broadcast_to(mass_ref[b : b + 1, :], (size, size)).T
        mass_col[at, :] = column
        own = padded[BAND + b].astype(F32)
        weights[at, width:] = (column * own).astype(BF16)

    def apply(source, store):
        for b in range(count):
            matrix = jnp.concatenate([blocks[b, n] for n in range(3)], axis=1)
            tiles = []
            for n in range(3):
                local = nb_ref[b, n] - place * count + BAND
                local = jnp.minimum(jnp.maximum(local, 0), count + 2 * BAND - 1)
                tiles.append(source[local])
            value = jnp.dot(
                matrix, jnp.concatenate(tiles, axis=0), preferred_element_type=F32
            )
            store(b, value)

    def store_image(b, value):
        weights[pl.ds(b * size, size), :width] = value.astype(BF16)

    load_blocks.wait()
    halo_low.wait_recv()
    halo_high.wait_recv()
    apply(padded, store_image)

    def add_gram(which, source, start, length, fresh):
        part = transposed_dot(source, weights[pl.ds(start * size, length * size), :])
        at = pl.ds(pl.multiple_of(col_of[which] * width, width), width)
        for j in range(2):
            value = part[:, j * width : (j + 1) * width]
            gram[j, at, :] = value if fresh else gram[j, at, :] + value

    def some(ref, start, length):
        return ref[pl.ds(start, length)].reshape(length * size, width)

    step = count // 4
    for i in range(4):
        add_gram(OWN, some(padded, BAND + i * step, step), i * step, step, i == 0)

    left_first.wait_recv()
    right_first.wait_recv()
    far_low, far_high = [], []
    for i in range(parts):
        at = pl.ds(i * piece, piece)
        far_low.append(
            send(
                others.at[0, at], others.at[2, at], y_send.at[4 + i], y_recv.at[4 + i], y_right
            )
        )
        at = pl.ds(half + i * piece, piece)
        j = 4 + parts + i
        far_high.append(
            send(others.at[1, at], others.at[2, at], y_send.at[j], y_recv.at[j], y_left)
        )
    left, right, far = (others.at[i] for i in range(3))
    for i in range(2):
        add_gram(LEFT, some(left, i * step, step), i * step, step, i == 0)
    for i in range(2, 4):
        add_gram(RIGHT, some(right, i * step, step), i * step, step, i == 2)
    for load in load_turn:
        load.wait()
    left_second.wait_recv()
    right_second.wait_recv()
    near = 3 * width
    for i in range(count // 2):
        joined = jnp.concatenate(
            [some(padded, BAND + 2 * i, 2), some(left, 2 * i, 2), some(right, 2 * i, 2)], axis=1
        )
        turned[pl.ds(2 * i * size, 2 * size), :] = jnp.dot(
            joined, turn[:near, :], preferred_element_type=F32
        )
    for i in range(2, 4):
        add_gram(LEFT, some(left, i * step, step), i * step, step, False)
    for i in range(2):
        add_gram(RIGHT, some(right, i * step, step), i * step, step, False)

    sums = jnp.zeros((8, width), F32)

    def far_turn(start, sums):
        at = pl.ds(start * size, piece * size)
        value = turned[at, :] + jnp.dot(
            some(far, start, piece), turn[near:, :], preferred_element_type=F32
        )
        turned[at, :] = value
        rimmed[pl.ds(BAND + start, piece)] = value.astype(BF16).reshape(piece, size, width)
        squares = mass_col[at, :] * value * value
        return sums + jnp.sum(squares.reshape(piece * size // 8, 8, width), axis=0)

    for i in range(parts):
        last = i == parts - 1
        far_low[i].wait_recv()
        far_high[i].wait_recv()
        for start in (i * piece, half + i * piece):
            sums = far_turn(start, sums)
        if last:
            sq_own[...] = jnp.sum(sums, axis=0, keepdims=True)
            sq_hop = send(sq_own, sq_core, core_send.at[1], core_recv.at[1], partner)
            rim_low = send(
                rimmed.at[last_rows], rimmed.at[before], halo_send.at[2], halo_recv.at[2], up
            )
            rim_high = send(
                rimmed.at[first_rows], rimmed.at[after], halo_send.at[3], halo_recv.at[3], down
            )
        for start in (i * piece, half + i * piece):
            add_gram(FAR, some(far, start, piece), start, piece, i == 0 and start == 0)

    gram_hop = send(gram.at[1 - k], gram_core, core_send.at[0], core_recv.at[0], partner)
    sq_hop.wait_recv()
    sq_x[...] = sq_own[...] + sq_core[...]
    sq_x_hops = [
        send(sq_x, sq_x_in.at[d], x_send.at[nx - 1 + d], x_recv.at[nx - 1 + d], peer)
        for d, peer in enumerate(x_peers)
    ]
    gram_hop.wait_recv()
    group = 8 * nx
    for i in range(nz):
        at = pl.ds(i * group, group)
        value = (gram[k, at, :] + gram_core[at, :]).reshape(nx, 8, width)
        for j in range(nx):
            gram_x[j, i] = value[j]
    gram_x_hops = [
        send(
            gram_x.at[lax.rem(x + 1 + d, nx)], gram_x_in.at[d], x_send.at[d], x_recv.at[d], peer
        )
        for d, peer in enumerate(x_peers)
    ]
    for hop in sq_x_hops:
        hop.wait_recv()
    value = sq_x[...]
    for d in range(nx - 1):
        value = value + sq_x_in[d]
    sq_z[...] = value
    sq_z_hops = [
        send(sq_z, sq_z_in.at[d], z_send.at[nz - 1 + d], z_recv.at[nz - 1 + d], peer)
        for d, peer in enumerate(z_peers)
    ]
    for hop in gram_x_hops:
        hop.wait_recv()
    value = gram_x[x]
    for d in range(nx - 1):
        value = value + gram_x_in[d]
    gram_z[...] = value
    gram_z_hops = [
        send(
            gram_z.at[lax.rem(z + 1 + d, nz)], gram_z_in.at[d], z_send.at[d], z_recv.at[d], peer
        )
        for d, peer in enumerate(z_peers)
    ]

    def store_product(b, value):
        product[pl.ds(b * size, size), :] = value

    rim_low.wait_recv()
    rim_high.wait_recv()
    apply(rimmed, store_product)

    for hop in sq_z_hops:
        hop.wait_recv()
    norm = sq_z[...]
    for d in range(nz - 1):
        norm = norm + sq_z_in[d]
    scale = lax.rsqrt(norm / vertices)

    for hop in gram_z_hops:
        hop.wait_recv()
    value = gram_z[z]
    for d in range(nz - 1):
        value = value + gram_z_in[d]
    tile_mine[...] = value / vertices
    tile_hop = send(tile_mine, tile_in, core_send.at[2], core_recv.at[2], partner)
    basis_out[...] = (turned[...] * scale).astype(BF16)
    image_out[...] = (product[...] * scale).astype(BF16)
    tile_hop.wait_recv()
    first = tile_mine[...]
    second = tile_in[...]
    stiff = jnp.where(k == 0, first, second)
    mass = jnp.where(k == 0, second, first)
    stiff_out[...] = jnp.where(k == 0, stiff[:4], stiff[4:])
    mass_out[...] = jnp.where(k == 0, mass[:4], mass[4:])
    for copy in started:
        copy.wait_send()


def body(basis_rows, stiff_blocks, block_neighbors, vertex_mass, rotation):
    nz, nx, _ = (lax.axis_size(a) for a in ROWS)
    ny = lax.axis_size("cols")
    rows, width = basis_rows.shape
    count, _, size, _ = stiff_blocks.shape
    parts = 2
    sizes = (nz, nx, ny, count, size, width, parts)
    reach = (count + 2 * BAND, size, width)
    vmem = pl.BlockSpec(memory_space=pltpu.VMEM)
    anywhere = pl.BlockSpec(memory_space=pl.ANY)
    dma = pltpu.SemaphoreType.DMA
    return pl.pallas_call(
        functools.partial(kernel, sizes),
        out_shape=(
            jax.ShapeDtypeStruct((rows, width), BF16),
            jax.ShapeDtypeStruct((rows, width), BF16),
            jax.ShapeDtypeStruct((4, width), F32),
            jax.ShapeDtypeStruct((4, width), F32),
        ),
        in_specs=[
            pl.BlockSpec(memory_space=pltpu.SMEM),
            anywhere,
            anywhere,
            vmem,
            anywhere,
        ],
        out_specs=(vmem, vmem, vmem, vmem),
        scratch_shapes=[
            pltpu.VMEM(reach, BF16),
            pltpu.VMEM((3, count, size, width), BF16),
            pltpu.VMEM(reach, BF16),
            pltpu.VMEM((rows, width), F32),
            pltpu.VMEM((rows, width), F32),
            pltpu.VMEM((rows, width), F32),
            pltpu.VMEM((rows, 2 * width), BF16),
            pltpu.VMEM(stiff_blocks.shape, BF16),
            pltpu.VMEM((ny * width, width), BF16),
            pltpu.VMEM((2, ny * width, width), F32),
            pltpu.VMEM((ny * width, width), F32),
            pltpu.VMEM((nx, nz, 8, width), F32),
            pltpu.VMEM((nx - 1, nz, 8, width), F32),
            pltpu.VMEM((nz, 8, width), F32),
            pltpu.VMEM((nz - 1, 8, width), F32),
            pltpu.VMEM((8, width), F32),
            pltpu.VMEM((8, width), F32),
            pltpu.VMEM((1, width), F32),
            pltpu.VMEM((1, width), F32),
            pltpu.VMEM((1, width), F32),
            pltpu.VMEM((nx - 1, 1, width), F32),
            pltpu.VMEM((1, width), F32),
            pltpu.VMEM((nz - 1, 1, width), F32),
            dma((2 + ny,)),
            dma((4 + 2 * parts,)),
            dma((4 + 2 * parts,)),
            dma((4,)),
            dma((4,)),
            dma((3,)),
            dma((3,)),
            dma((2 * (nx - 1),)),
            dma((2 * (nx - 1),)),
            dma((2 * (nz - 1),)),
            dma((2 * (nz - 1),)),
        ],
        compiler_params=pltpu.CompilerParams(collective_id=0, has_side_effects=True),
    )(
        block_neighbors,
        basis_rows.reshape(count, size, width),
        stiff_blocks,
        vertex_mass.reshape(count, size),
        rotation,
    )


def solution(mesh):
    split = Mesh(
        mesh.devices.reshape(16, 4, 2, mesh.shape["cols"]), ("rows_0", "rows_1", "rows_2", "cols")
    )
    in_specs = (P(ROWS, "cols"), P(ROWS, None, None, None), P(ROWS, None), P(ROWS), P())
    out_specs = (P(ROWS, "cols"), P(ROWS, "cols"), P(ROWS, "cols"), P(ROWS, "cols"))
    return jax.shard_map(body, mesh=split, in_specs=in_specs, out_specs=out_specs, check_vma=False)
```

time: 139 us -> 68.9 us (0.50)
  Pallas kernels: 0 us -> 61.5 us
  blocking collectives: 60.8 us -> 0 us
  starting transfers between devices: 22.4 us -> 0 us
  waiting for transfers between devices: 13.8 us -> 0 us
  matrix products: 12.5 us -> 0 us
  local copies, waits for them, and re-layouts: 18.4 us -> 6.46 us
  other arithmetic: 9.13 us -> 0 us
    pallas_call x0 -> x1, Pallas kernels: none -> 61.5 us  [body(): pl.pallas_call(functools.partial(kernel, sizes), out_shape=(jax.ShapeDtyp...]
    all_to_all x2 -> x0, blocking collectives: 60.8 us -> none  [the longest x1 49.2 us: body(): lax.all_to_all(nearer, far, split_axis=0, concat_axis=0, tiled=True)]
    ppermute x4 -> x0, starting transfers between devices: 17.3 us -> none  [the longest x2 9.81 us: with_halo(): lax.ppermute(lax.slice_in_dim(block, block.shape[dim] - width, None, axis...]
    dot_general x5 -> x0, matrix products: 12.5 us -> none  [the longest x2 4.5 us: apply_blocks(): jnp.einsum('knij,knjc->kic', stiff_blocks, source, preferred_element_type...]
    all_to_all x1 -> x0, waiting for transfers between devices: 8.49 us -> none  [from_everyone(): lax.all_to_all(jnp.broadcast_to(value[None], (size, *value.shape)), axis,...]
    ppermute x4 -> x0, waiting for transfers between devices: 5.3 us -> none  [the longest x2 5.29 us: with_halo(): lax.ppermute(lax.slice_in_dim(block, 0, width, axis=dim), axis, backward)]
    all_to_all x1 -> x0, starting transfers between devices: 5.13 us -> none  [from_everyone(): lax.all_to_all(jnp.broadcast_to(value[None], (size, *value.shape)), axis,...]
    gather x2 -> x0, local copies, waits for them, and re-layouts: 4.24 us -> none  [apply_blocks(): source = tiles[local_index]]
  transfers between devices with their start and end apart: 5 -> 0, of which waited for: 3 -> 0; matrix products, arithmetic and copies ran while one was open for 6% -> 0% of each run, Pallas kernels for 0% -> 0%
where the time goes in v2:
time: 68.9 us; the launch traced here: 68.6 us
  Pallas kernels  61.5 us (89%)
  local copies, waits for them, and re-layouts  6.46 us (9%)
    pallas_call x1, Pallas kernels, body(): pl.pallas_call(functools.partial(kernel, sizes), out_shape=(jax.ShapeDtyp...  61.5 us
    unnamed x9, local copies, waits for them, and re-layouts  6.46 us

profile of v2, /device:TPU:1, one launch (start us, length us, event | category | flops | bytes accessed | tf_op | source)
XLA Modules:
  0.0 68.6 jit_solution(14029394032334069065)
XLA Ops:
  0.6 1.4 %copy.9.nb_ref = s32[20,3]{1,0:T(8,128)} copy(s32[20,3]{0,1:T(4,128)} %param.7) | data formatting | bytes 480 | tf_op args[2]
  2.0 61.5 %shard_map.84 = (bf16[2560,128]{1,0:T(8,128)(2,1)}, bf16[2560,128]{1,0:T(8,128)(2,1)}, f32[4,128]{1,0:T(4,128)}, f32[4,128]{1,0:T(4,128)}) custom-call(s32[20,3]{1,0:T(8,128)} %copy.9.nb_ref, bf16[20,128,128]{2,1,0:T(8,128)(2,1)} %bitcast.2, bf16[20,3,128,128]{3,2,1,0:T(8,128)(2,1)} %blocks_ref.1, f32[20,128]{1,0:T(8,128)} %bitcast.3, bf16[512,512]{1,0:T(8,128)(2,1)} %rot_ref.1), custom_call_target="tpu_custom_call" | custom-call | tf_op jit(solution)/shard_map/pallas_call | solution.py:353
  63.5 0.0 copy-start.1
  63.5 0.0 copy-start
  63.5 2.0 %copy.14 = bf16[2560,128]{1,0:T(8,128)(2,1)} copy(bf16[2560,128]{1,0:T(8,128)(2,1)} %get-tuple-element.8) | data formatting | bytes 1310720
  65.5 2.0 %copy.15 = bf16[2560,128]{1,0:T(8,128)(2,1)} copy(bf16[2560,128]{1,0:T(8,128)(2,1)} %get-tuple-element.9) | data formatting | bytes 1310720
  67.5 0.0 copy-done.1
  67.5 0.6 copy.16
  68.0 0.0 copy-done
  68.0 0.6 copy.17
Async XLA Ops:
  63.5 4.0 %copy-start.1 = (f32[4,128]{1,0:T(4,128)S(1)}, f32[4,128]{1,0:T(4,128)}, u32[]{:S(2)}) copy-start(f32[4,128]{1,0:T(4,128)} %get-tuple-element.10) | copy-start | bytes 6148
  63.5 4.5 %copy-start = (f32[4,128]{1,0:T(4,128)S(1)}, f32[4,128]{1,0:T(4,128)}, u32[]{:S(2)}) copy-start(f32[4,128]{1,0:T(4,128)} %get-tuple-element.11) | copy-start | bytes 6148

commit v3 on v2

v3 whole, which is shorter than its diff:
```python
import functools

import jax
import jax.numpy as jnp
from jax import lax
from jax.experimental import pallas as pl
from jax.experimental.pallas import tpu as pltpu
from jax.sharding import Mesh
from jax.sharding import PartitionSpec as P

BAND = 8
ROWS = ("rows_0", "rows_1", "rows_2")
MESH = pl.DeviceIdType.MESH
F32 = jnp.float32
BF16 = jnp.bfloat16
LEFT, OWN, RIGHT, FAR = 0, 1, 2, 3
VMEM_LIMIT = 24 * 1024 * 1024
FINISH_LIMIT = 16 * 1024 * 1024


def transposed_dot(left, right):
    return lax.dot_general(left, right, (((0,), (0,)), ((), ())), preferred_element_type=F32)


def kernel(
    sizes,
    nb_ref,
    basis_ref,
    blocks_ref,
    mass_hbm,
    rot_ref,
    turned,
    product,
    scale_out,
    gram_out,
    padded,
    others,
    rimmed,
    mass_ref,
    mass_col,
    weights,
    blocks,
    turn,
    gram,
    plane,
    plane_in,
    line,
    line_in,
    sq_own,
    sq_plane_in,
    sq_line,
    sq_line_in,
    relay,
    load_sem,
    y_send,
    y_recv,
    halo_send,
    halo_recv,
    p_send,
    p_recv,
    z_send,
    z_recv,
):
    nz, nx, ny, count, size, width, parts = sizes
    z, x, k = (lax.axis_index(a) for a in ROWS)
    y = lax.axis_index("cols")
    half = count // 2
    piece = half // parts
    total = nz * nx * 2
    nq = 2 * nx
    q = 2 * x + k
    place = z * nq + q
    vertices = total * count * size
    slots = nz // ny
    early = nz - slots

    def row_device(index):
        index = lax.rem(index + total, total)
        return {
            "rows_0": lax.div(index, nq),
            "rows_1": lax.rem(lax.div(index, 2), nx),
            "rows_2": lax.rem(index, 2),
        }

    def along(axis, mine, length, step):
        return {axis: lax.rem(mine + length + step, length)}

    up, down = row_device(place + 1), row_device(place - 1)
    y_right, y_left = along("cols", y, ny, 1), along("cols", y, ny, -1)
    partner = {"rows_2": 1 - k}
    x_near = [along("rows_1", x, nx, d) for d in (1, -1)]
    z_near = [along("rows_0", z, nz, d) for d in (1, -1)]
    places = [lax.rem(q + d, nq) for d in range(1, nq)]
    q_peers = [{"rows_1": lax.div(p, 2), "rows_2": lax.rem(p, 2)} for p in places]
    z_peers = [along("rows_0", z, nz, d) for d in range(1, nz)]
    col_of = [lax.rem(y + ny - 1 + i, ny) for i in range(ny)]

    load_basis = pltpu.make_async_copy(basis_ref, padded.at[pl.ds(BAND, count)], load_sem.at[0])
    load_basis.start()
    load_mass = pltpu.make_async_copy(mass_hbm, mass_ref, load_sem.at[2 + ny])
    load_mass.start()

    peers = [y_right, y_left, partner, *x_near, *z_near]
    barrier = pltpu.get_barrier_semaphore()
    for peer in peers:
        pl.semaphore_signal(barrier, inc=1, device_id=peer, device_id_type=MESH)
    load_blocks = pltpu.make_async_copy(blocks_ref, blocks, load_sem.at[1])
    load_blocks.start()
    load_turn = []
    for i in range(ny):
        load = pltpu.make_async_copy(
            rot_ref.at[
                pl.ds(pl.multiple_of(col_of[i] * width, width), width),
                pl.ds(pl.multiple_of(y * width, width), width),
            ],
            turn.at[pl.ds(i * width, width)],
            load_sem.at[2 + i],
        )
        load.start()
        load_turn.append(load)
    load_basis.wait()
    pl.semaphore_wait(barrier, len(peers))

    started = []

    def send(source, target, send_sem, recv_sem, device):
        copy = pltpu.make_async_remote_copy(
            src_ref=source,
            dst_ref=target,
            send_sem=send_sem,
            recv_sem=recv_sem,
            device_id=device,
            device_id_type=MESH,
        )
        copy.start()
        started.append(copy)
        return copy

    low, high = pl.ds(0, half), pl.ds(half, half)
    mine_low, mine_high = pl.ds(BAND, half), pl.ds(BAND + half, half)
    left_first = send(
        padded.at[mine_low], others.at[0, low], y_send.at[0], y_recv.at[0], y_right
    )
    right_first = send(
        padded.at[mine_high], others.at[1, high], y_send.at[1], y_recv.at[1], y_left
    )
    left_second = send(
        padded.at[mine_high], others.at[0, high], y_send.at[2], y_recv.at[2], y_right
    )
    right_second = send(
        padded.at[mine_low], others.at[1, low], y_send.at[3], y_recv.at[3], y_left
    )

    relays = [
        [*z_near, *x_near, partner],
        [z_peers[1], z_peers[nz - 3], *x_near, partner],
        [z_peers[3], z_peers[nz - 5]],
    ]

    def tell(i):
        for peer in relays[i]:
            pl.semaphore_signal(relay.at[i], inc=1, device_id=peer, device_id_type=MESH)

    def hear(i):
        pl.semaphore_wait(relay.at[i], len(relays[i]))

    def weigh(b):
        at = pl.ds(b * size, size)
        column = jnp.broadcast_to(mass_ref[b : b + 1, :], (size, size)).T
        mass_col[at, :] = column
        weights[at, width:] = (column * padded[BAND + b].astype(F32)).astype(BF16)

    tell(0)
    load_mass.wait()
    for b in range(half):
        weigh(b)
    hear(0)
    tell(1)
    for b in range(half, count):
        weigh(b)
    hear(1)
    first_rows, last_rows = pl.ds(BAND, BAND), pl.ds(count, BAND)
    before, after = pl.ds(0, BAND), pl.ds(BAND + count, BAND)
    halo_low = send(
        padded.at[last_rows], padded.at[before], halo_send.at[0], halo_recv.at[0], up
    )
    halo_high = send(
        padded.at[first_rows], padded.at[after], halo_send.at[1], halo_recv.at[1], down
    )
    tell(2)

    def apply(source, store):
        for b in range(count):
            matrix = jnp.concatenate([blocks[b, n] for n in range(3)], axis=1)
            tiles = []
            for n in range(3):
                local = nb_ref[n, b] - place * count + BAND
                local = jnp.minimum(jnp.maximum(local, 0), count + 2 * BAND - 1)
                tiles.append(source[local])
            value = jnp.dot(
                matrix, jnp.concatenate(tiles, axis=0), preferred_element_type=F32
            )
            store(b, value)

    def store_image(b, value):
        weights[pl.ds(b * size, size), :width] = value.astype(BF16)

    load_blocks.wait()
    halo_low.wait_recv()
    halo_high.wait_recv()
    apply(padded, store_image)
    hear(2)

    def add_gram(which, source, start, length, fresh):
        part = transposed_dot(source, weights[pl.ds(start * size, length * size), :])
        for j in range(2):
            value = part[:, j * width : (j + 1) * width]
            gram[which, j] = value if fresh else gram[which, j] + value

    def some(ref, start, length):
        return ref[pl.ds(start, length)].reshape(length * size, width)

    step = count // 4
    for i in range(4):
        add_gram(OWN, some(padded, BAND + i * step, step), i * step, step, i == 0)

    left_first.wait_recv()
    right_first.wait_recv()
    chunks = []
    far_low, far_high = [], []
    for i in range(parts):
        starts = (i * piece, count - (i + 1) * piece)
        chunks.append(starts)
        at = pl.ds(starts[0], piece)
        j = 4 + i
        far_low.append(
            send(others.at[0, at], others.at[2, at], y_send.at[j], y_recv.at[j], y_right)
        )
        at = pl.ds(starts[1], piece)
        j = 4 + parts + i
        far_high.append(
            send(others.at[1, at], others.at[2, at], y_send.at[j], y_recv.at[j], y_left)
        )
    left, right, far = (others.at[i] for i in range(3))
    for i in range(2):
        add_gram(LEFT, some(left, i * step, step), i * step, step, i == 0)
    for i in range(2, 4):
        add_gram(RIGHT, some(right, i * step, step), i * step, step, i == 2)
    for load in load_turn:
        load.wait()
    left_second.wait_recv()
    right_second.wait_recv()
    for i in range(2, 4):
        add_gram(LEFT, some(left, i * step, step), i * step, step, False)
    for i in range(2):
        add_gram(RIGHT, some(right, i * step, step), i * step, step, False)

    def pack(which):
        for t in range(width // 8):
            for j in range(2):
                value = gram[which, j, pl.ds(8 * t, 8), :]
                at = slots * which + t // nx
                plane[2 * (t % nx), at, j] = value[:4]
                plane[2 * (t % nx) + 1, at, j] = value[4:]

    def plane_sends(at, offset):
        return [
            send(
                plane.at[places[d], at],
                plane_in.at[d, at],
                p_send.at[offset + d],
                p_recv.at[offset + d],
                peer,
            )
            for d, peer in enumerate(q_peers)
        ]

    def plane_sum(at):
        value = plane[q, at]
        for d in range(nq - 1):
            value = value + plane_in[d, at]
        line[at] = value

    for which in (LEFT, OWN, RIGHT):
        pack(which)
    early_at, late_at = pl.ds(0, early), pl.ds(early, slots)
    early_hops = plane_sends(early_at, 0)
    near = 3 * width
    for i in range(count // 2):
        joined = jnp.concatenate(
            [some(left, 2 * i, 2), some(padded, BAND + 2 * i, 2), some(right, 2 * i, 2)], axis=1
        )
        turned[pl.ds(2 * i * size, 2 * size), :] = jnp.dot(
            joined, turn[:near, :], preferred_element_type=F32
        )

    sums = jnp.zeros((8, width), F32)

    def far_turn(start, sums):
        at = pl.ds(start * size, piece * size)
        value = turned[at, :] + jnp.dot(
            some(far, start, piece), turn[near:, :], preferred_element_type=F32
        )
        turned[at, :] = value
        rimmed[pl.ds(BAND + start, piece)] = value.astype(BF16).reshape(piece, size, width)
        squares = mass_col[at, :] * value * value
        return sums + jnp.sum(squares.reshape(piece * size // 8, 8, width), axis=0)

    rims = []
    quarter = BAND // 2
    for i in range(parts):
        far_low[i].wait_recv()
        far_high[i].wait_recv()
        for start in chunks[i]:
            sums = far_turn(start, sums)
        if (i + 1) * piece % quarter == 0 and (i + 1) * piece <= BAND:
            done = (i + 1) * piece
            j = 2 + 2 * (done // quarter - 1)
            rims.append(
                send(
                    rimmed.at[pl.ds(BAND + done - quarter, quarter)],
                    rimmed.at[pl.ds(BAND + count + done - quarter, quarter)],
                    halo_send.at[j],
                    halo_recv.at[j],
                    down,
                )
            )
            rims.append(
                send(
                    rimmed.at[pl.ds(BAND + count - done, quarter)],
                    rimmed.at[pl.ds(BAND - done, quarter)],
                    halo_send.at[j + 1],
                    halo_recv.at[j + 1],
                    up,
                )
            )
        if i == parts - 2:
            for hop in early_hops:
                hop.wait_recv()
            plane_sum(early_at)
        if i == parts - 1:
            sq_own[...] = jnp.sum(sums, axis=0, keepdims=True)
            sq_hops = [
                send(
                    sq_own,
                    sq_plane_in.at[d],
                    p_send.at[2 * (nq - 1) + d],
                    p_recv.at[2 * (nq - 1) + d],
                    peer,
                )
                for d, peer in enumerate(q_peers)
            ]
        for j, start in enumerate(chunks[i]):
            add_gram(FAR, some(far, start, piece), start, piece, i == 0 and j == 0)

    pack(FAR)
    late_hops = plane_sends(late_at, nq - 1)
    for hop in sq_hops:
        hop.wait_recv()
    value = sq_own[...]
    for d in range(nq - 1):
        value = value + sq_plane_in[d]
    sq_line[...] = value
    sq_line_hops = [
        send(sq_line, sq_line_in.at[d], z_send.at[nz - 1 + d], z_recv.at[nz - 1 + d], peer)
        for d, peer in enumerate(z_peers)
    ]
    for hop in late_hops:
        hop.wait_recv()
    plane_sum(late_at)
    base = z + slots + nz - slots * y
    line_hops = [
        send(
            line.at[lax.rem(base + 1 + d, nz)], line_in.at[d], z_send.at[d], z_recv.at[d], peer
        )
        for d, peer in enumerate(z_peers)
    ]

    def store_product(b, value):
        product[pl.ds(b * size, size), :] = value

    for hop in rims:
        hop.wait_recv()
    apply(rimmed, store_product)

    for hop in sq_line_hops:
        hop.wait_recv()
    norm = sq_line[...]
    for d in range(nz - 1):
        norm = norm + sq_line_in[d]
    scale_out[...] = lax.rsqrt(norm / vertices)
    for hop in line_hops:
        hop.wait_recv()
    value = line[lax.rem(base, nz)]
    for d in range(nz - 1):
        value = value + line_in[d]
    gram_out[...] = value / vertices
    for copy in started:
        copy.wait_send()


def finish(
    turned, product, scale, gram, basis_out, image_out, stiff_out, mass_out, basis, image, sem
):
    rows = turned.shape[0]
    pieces = 4
    step = rows // pieces
    copies = []
    stiff_out[...] = gram[0]
    mass_out[...] = gram[1]
    for i in range(pieces):
        at = pl.ds(i * step, step)
        for j, (source, held, target) in enumerate(
            ((turned, basis, basis_out), (product, image, image_out))
        ):
            held[at, :] = (source[at, :] * scale[...]).astype(BF16)
            copy = pltpu.make_async_copy(held.at[at], target.at[at], sem.at[2 * i + j])
            copy.start()
            copies.append(copy)
    for copy in copies:
        copy.wait()


def in_hbm(value):
    return pltpu.with_memory_space_constraint(value, pltpu.HBM)


def body(basis_rows, stiff_blocks, block_neighbors, vertex_mass, rotation):
    nz, nx, _ = (lax.axis_size(a) for a in ROWS)
    ny = lax.axis_size("cols")
    rows, width = basis_rows.shape
    count, _, size, _ = stiff_blocks.shape
    parts = 5
    nq = 2 * nx
    sizes = (nz, nx, ny, count, size, width, parts)
    reach = (count + 2 * BAND, size, width)
    vmem = pl.BlockSpec(memory_space=pltpu.VMEM)
    hbm = pl.BlockSpec(memory_space=pltpu.HBM)
    dma = pltpu.SemaphoreType.DMA
    turned, product, scale, gram = pl.pallas_call(
        functools.partial(kernel, sizes),
        out_shape=(
            jax.ShapeDtypeStruct((rows, width), F32),
            jax.ShapeDtypeStruct((rows, width), F32),
            jax.ShapeDtypeStruct((1, width), F32),
            jax.ShapeDtypeStruct((2, 4, width), F32),
        ),
        in_specs=[pl.BlockSpec(memory_space=pltpu.SMEM), hbm, hbm, hbm, hbm],
        out_specs=(vmem, vmem, vmem, vmem),
        scratch_shapes=[
            pltpu.VMEM(reach, BF16),
            pltpu.VMEM((3, count, size, width), BF16),
            pltpu.VMEM(reach, BF16),
            pltpu.VMEM((count, size), F32),
            pltpu.VMEM((rows, width), F32),
            pltpu.VMEM((rows, 2 * width), BF16),
            pltpu.VMEM(stiff_blocks.shape, BF16),
            pltpu.VMEM((ny * width, width), BF16),
            pltpu.VMEM((ny, 2, width, width), F32),
            pltpu.VMEM((nq, nz, 2, 4, width), F32),
            pltpu.VMEM((nq - 1, nz, 2, 4, width), F32),
            pltpu.VMEM((nz, 2, 4, width), F32),
            pltpu.VMEM((nz - 1, 2, 4, width), F32),
            pltpu.VMEM((1, width), F32),
            pltpu.VMEM((nq - 1, 1, width), F32),
            pltpu.VMEM((1, width), F32),
            pltpu.VMEM((nz - 1, 1, width), F32),
            pltpu.SemaphoreType.REGULAR((3,)),
            dma((3 + ny,)),
            dma((4 + 2 * parts,)),
            dma((4 + 2 * parts,)),
            dma((6,)),
            dma((6,)),
            dma((3 * (nq - 1),)),
            dma((3 * (nq - 1),)),
            dma((2 * (nz - 1),)),
            dma((2 * (nz - 1),)),
        ],
        compiler_params=pltpu.CompilerParams(
            collective_id=0, has_side_effects=True, vmem_limit_bytes=VMEM_LIMIT
        ),
    )(
        in_hbm(block_neighbors.T),
        in_hbm(basis_rows.reshape(count, size, width)),
        in_hbm(stiff_blocks),
        in_hbm(vertex_mass.reshape(count, size)),
        in_hbm(rotation),
    )
    return pl.pallas_call(
        finish,
        out_shape=(
            jax.ShapeDtypeStruct((rows, width), BF16),
            jax.ShapeDtypeStruct((rows, width), BF16),
            jax.ShapeDtypeStruct((4, width), F32),
            jax.ShapeDtypeStruct((4, width), F32),
        ),
        in_specs=[vmem] * 4,
        out_specs=(hbm, hbm, vmem, vmem),
        scratch_shapes=[
            pltpu.VMEM((rows, width), BF16),
            pltpu.VMEM((rows, width), BF16),
            dma((8,)),
        ],
        compiler_params=pltpu.CompilerParams(vmem_limit_bytes=FINISH_LIMIT),
    )(turned, product, scale, gram)


def solution(mesh):
    split = Mesh(
        mesh.devices.reshape(16, 4, 2, mesh.shape["cols"]), ("rows_0", "rows_1", "rows_2", "cols")
    )
    in_specs = (P(ROWS, "cols"), P(ROWS, None, None, None), P(ROWS, None), P(ROWS), P())
    out_specs = (P(ROWS, "cols"), P(ROWS, "cols"), P(ROWS, "cols"), P(ROWS, "cols"))
    return jax.shard_map(body, mesh=split, in_specs=in_specs, out_specs=out_specs, check_vma=False)
```

time: 68.9 us -> 56.8 us (0.82)
  local copies, waits for them, and re-layouts: 6.46 us -> 0 us
  Pallas kernels: 61.5 us -> 56 us
    pallas_call x1, Pallas kernels: 61.5 us -> 54.2 us  [body(): pl.pallas_call(functools.partial(kernel, sizes), out_shape=(jax.ShapeDtyp...]
    unnamed x9 -> x0, local copies, waits for them, and re-layouts: 6.46 us -> none
    pallas_call x0 -> x1, Pallas kernels: none -> 1.72 us  [body(): pl.pallas_call(finish, out_shape=(jax.ShapeDtypeStruct((rows, width), BF1...]
where the time goes in v3:
time: 56.8 us; the launch traced here: 56.6 us
  Pallas kernels  56 us (99%)
  between operations  0.64 us (1%)
    pallas_call x1, Pallas kernels, body(): pl.pallas_call(functools.partial(kernel, sizes), out_shape=(jax.ShapeDtyp...  54.2 us
    pallas_call x1, Pallas kernels, body(): pl.pallas_call(finish, out_shape=(jax.ShapeDtypeStruct((rows, width), BF1...  1.72 us

profile of v3, /device:TPU:1, one launch (start us, length us, event | category | flops | bytes accessed | tf_op | source)
XLA Modules:
  0.0 56.6 jit_solution(12068079404919148129)
XLA Ops:
  0.6 54.2 %shard_map.84 = (f32[2560,128]{1,0:T(8,128)S(1)}, f32[2560,128]{1,0:T(8,128)S(1)}, f32[1,128]{1,0:T(1,128)S(1)}, f32[2,4,128]{2,1,0:T(4,128)S(1)}) custom-call(s32[3,20]{1,0:T(4,128)} %bitcast.5, bf16[20,128,128]{2,1,0:T(8,128)(2,1)} %bitcast.3, bf16[20,3,128,128]{3,2,1,0:T(8,128)(2,1)} %blocks_ref.1, f32[20,128]{1,0:T(8,128)} %bitcast.4, ...), custom_call_target="tpu_custom_call" | custom-call | tf_op jit(solution)/shard_map/pallas_call | solution.py:440
  54.9 1.7 %shard_map.85 = (bf16[2560,128]{1,0:T(8,128)(2,1)}, bf16[2560,128]{1,0:T(8,128)(2,1)}, f32[4,128]{1,0:T(4,128)}, f32[4,128]{1,0:T(4,128)}) custom-call(f32[2560,128]{1,0:T(8,128)S(1)} %get-tuple-element.8.turned, f32[2560,128]{1,0:T(8,128)S(1)} %get-tuple-element.9.product, f32[1,128]{1,0:T(1,128)S(1)} %get-tuple-element.10.scale, ...), custom_call_target="tpu_custom_call" | custom-call | tf_op jit(solution)/shard_map/pallas_call | solution.py:489

commit v4 on v3

--- a/solution.py
+++ b/solution.py
@@ -97,7 +97,7 @@
 
     load_basis = pltpu.make_async_copy(basis_ref, padded.at[pl.ds(BAND, count)], load_sem.at[0])
     load_basis.start()
-    load_mass = pltpu.make_async_copy(mass_hbm, mass_ref, load_sem.at[2 + ny])
+    load_mass = pltpu.make_async_copy(mass_hbm, mass_ref, load_sem.at[3 + ny])
     load_mass.start()
 
     peers = [y_right, y_left, partner, *x_near, *z_near]
@@ -107,10 +107,10 @@
     load_blocks = pltpu.make_async_copy(blocks_ref, blocks, load_sem.at[1])
     load_blocks.start()
     load_turn = []
-    for i in range(ny):
+    for i in range(ny + 1):
         load = pltpu.make_async_copy(
             rot_ref.at[
-                pl.ds(pl.multiple_of(col_of[i] * width, width), width),
+                pl.ds(pl.multiple_of(col_of[i % ny] * width, width), width),
                 pl.ds(pl.multiple_of(y * width, width), width),
             ],
             turn.at[pl.ds(i * width, width)],
@@ -224,6 +224,36 @@
     for i in range(4):
         add_gram(OWN, some(padded, BAND + i * step, step), i * step, step, i == 0)
 
+    def pack(which):
+        for t in range(width // 8):
+            for j in range(2):
+                value = gram[which, j, pl.ds(8 * t, 8), :]
+                at = slots * which + t // nx
+                plane[2 * (t % nx), at, j] = value[:4]
+                plane[2 * (t % nx) + 1, at, j] = value[4:]
+
+    def plane_sends(at, offset):
+        return [
+            send(
+                plane.at[places[d], at],
+                plane_in.at[d, at],
+                p_send.at[offset + d],
+                p_recv.at[offset + d],
+                peer,
+            )
+            for d, peer in enumerate(q_peers)
+        ]
+
+    def plane_sum(at):
+        value = plane[q, at]
+        for d in range(nq - 1):
+            value = value + plane_in[d, at]
+        line[at] = value
+
+    at_piece = [pl.ds(slots * i, slots) for i in range(ny)]
+    pack(OWN)
+    early_hops = plane_sends(at_piece[OWN], 0)
+
     left_first.wait_recv()
     right_first.wait_recv()
     chunks = []
@@ -248,6 +278,15 @@
         add_gram(RIGHT, some(right, i * step, step), i * step, step, i == 2)
     for load in load_turn:
         load.wait()
+    for i in range(count // 2):
+        own = some(padded, BAND + 2 * i, 2)
+        if 2 * i < half:
+            pair, at = [some(left, 2 * i, 2), own], pl.ds(0, 2 * width)
+        else:
+            pair, at = [own, some(right, 2 * i, 2)], pl.ds(width, 2 * width)
+        turned[pl.ds(2 * i * size, 2 * size), :] = jnp.dot(
+            jnp.concatenate(pair, axis=1), turn[at, :], preferred_element_type=F32
+        )
     left_second.wait_recv()
     right_second.wait_recv()
     for i in range(2, 4):
@@ -255,51 +294,23 @@
     for i in range(2):
         add_gram(RIGHT, some(right, i * step, step), i * step, step, False)
 
-    def pack(which):
-        for t in range(width // 8):
-            for j in range(2):
-                value = gram[which, j, pl.ds(8 * t, 8), :]
-                at = slots * which + t // nx
-                plane[2 * (t % nx), at, j] = value[:4]
-                plane[2 * (t % nx) + 1, at, j] = value[4:]
-
-    def plane_sends(at, offset):
-        return [
-            send(
-                plane.at[places[d], at],
-                plane_in.at[d, at],
-                p_send.at[offset + d],
-                p_recv.at[offset + d],
-                peer,
-            )
-            for d, peer in enumerate(q_peers)
-        ]
-
-    def plane_sum(at):
-        value = plane[q, at]
-        for d in range(nq - 1):
-            value = value + plane_in[d, at]
-        line[at] = value
-
-    for which in (LEFT, OWN, RIGHT):
-        pack(which)
-    early_at, late_at = pl.ds(0, early), pl.ds(early, slots)
-    early_hops = plane_sends(early_at, 0)
-    near = 3 * width
-    for i in range(count // 2):
-        joined = jnp.concatenate(
-            [some(left, 2 * i, 2), some(padded, BAND + 2 * i, 2), some(right, 2 * i, 2)], axis=1
-        )
-        turned[pl.ds(2 * i * size, 2 * size), :] = jnp.dot(
-            joined, turn[:near, :], preferred_element_type=F32
-        )
+    pack(LEFT)
+    early_hops += plane_sends(at_piece[LEFT], nq - 1)
+    pack(RIGHT)
+    early_hops += plane_sends(at_piece[RIGHT], 2 * (nq - 1))
 
     sums = jnp.zeros((8, width), F32)
 
     def far_turn(start, sums):
         at = pl.ds(start * size, piece * size)
+        if start < half:
+            pair, place_of = [some(right, start, piece), some(far, start, piece)], 2
+        else:
+            pair, place_of = [some(far, start, piece), some(left, start, piece)], 3
         value = turned[at, :] + jnp.dot(
-            some(far, start, piece), turn[near:, :], preferred_element_type=F32
+            jnp.concatenate(pair, axis=1),
+            turn[pl.ds(place_of * width, 2 * width), :],
+            preferred_element_type=F32,
         )
         turned[at, :] = value
         rimmed[pl.ds(BAND + start, piece)] = value.astype(BF16).reshape(piece, size, width)
@@ -308,53 +319,83 @@
 
     rims = []
     quarter = BAND // 2
-    for i in range(parts):
+    def send_rims(done):
+        j = 2 + 2 * (done // quarter - 1)
+        rims.append(
+            send(
+                rimmed.at[pl.ds(BAND + done - quarter, quarter)],
+                rimmed.at[pl.ds(BAND + count + done - quarter, quarter)],
+                halo_send.at[j],
+                halo_recv.at[j],
+                down,
+            )
+        )
+        rims.append(
+            send(
+                rimmed.at[pl.ds(BAND + count - done, quarter)],
+                rimmed.at[pl.ds(BAND - done, quarter)],
+                halo_send.at[j + 1],
+                halo_recv.at[j + 1],
+                up,
+            )
+        )
+
+    def far_gram(i):
+        for j, start in enumerate(chunks[i]):
+            add_gram(FAR, some(far, start, piece), start, piece, i == 0 and j == 0)
+
+    slot_of = [lax.rem(z + d + slots + nz - slots * y, nz) for d in range(nz)]
+    line_copies = [
+        pltpu.make_async_remote_copy(
+            src_ref=line.at[slot_of[d + 1]],
+            dst_ref=line_in.at[d],
+            send_sem=z_send.at[d],
+            recv_sem=z_recv.at[d],
+            device_id=peer,
+            device_id_type=MESH,
+        )
+        for d, peer in enumerate(z_peers)
+    ]
+    far_first = sorted(range(nz - 1), key=lambda d: abs(d + 1 - nz // 2))
+
+    for i in range(parts - 1):
         far_low[i].wait_recv()
         far_high[i].wait_recv()
         for start in chunks[i]:
             sums = far_turn(start, sums)
         if (i + 1) * piece % quarter == 0 and (i + 1) * piece <= BAND:
-            done = (i + 1) * piece
-            j = 2 + 2 * (done // quarter - 1)
-            rims.append(
-                send(
-                    rimmed.at[pl.ds(BAND + done - quarter, quarter)],
-                    rimmed.at[pl.ds(BAND + count + done - quarter, quarter)],
-                    halo_send.at[j],
-                    halo_recv.at[j],
-                    down,
-                )
-            )
-            rims.append(
-                send(
-                    rimmed.at[pl.ds(BAND + count - done, quarter)],
-                    rimmed.at[pl.ds(BAND - done, quarter)],
-                    halo_send.at[j + 1],
-                    halo_recv.at[j + 1],
-                    up,
-                )
-            )
-        if i == parts - 2:
-            for hop in early_hops:
-                hop.wait_recv()
-            plane_sum(early_at)
-        if i == parts - 1:
-            sq_own[...] = jnp.sum(sums, axis=0, keepdims=True)
-            sq_hops = [
-                send(
-                    sq_own,
-                    sq_plane_in.at[d],
-                    p_send.at[2 * (nq - 1) + d],
-                    p_recv.at[2 * (nq - 1) + d],
-                    peer,
-                )
-                for d, peer in enumerate(q_peers)
-            ]
-        for j, start in enumerate(chunks[i]):
-            add_gram(FAR, some(far, start, piece), start, piece, i == 0 and j == 0)
-
+            send_rims((i + 1) * piece)
+        far_gram(i)
+    early_at, late_at = pl.ds(0, early), pl.ds(early, slots)
+    for hop in early_hops:
+        hop.wait_recv()
+    plane_sum(early_at)
+    for d in far_first:
+        pl.when(slot_of[d + 1] < early)(line_copies[d].start)
+    last = parts - 1
+    far_low[last].wait_recv()
+    far_high[last].wait_recv()
+    far_gram(last)
     pack(FAR)
-    late_hops = plane_sends(late_at, nq - 1)
+    late_hops = plane_sends(late_at, 3 * (nq - 1))
+    for start in chunks[last]:
+        sums = far_turn(start, sums)
+    sq_own[...] = jnp.sum(sums, axis=0, keepdims=True)
+    sq_hops = [
+        send(
+            sq_own,
+            sq_plane_in.at[d],
+            p_send.at[4 * (nq - 1) + d],
+            p_recv.at[4 * (nq - 1) + d],
+            peer,
+        )
+        for d, peer in enumerate(q_peers)
+    ]
+    for hop in late_hops:
+        hop.wait_recv()
+    plane_sum(late_at)
+    for d in far_first:
+        pl.when(slot_of[d + 1] >= early)(line_copies[d].start)
     for hop in sq_hops:
         hop.wait_recv()
     value = sq_own[...]
@@ -365,17 +406,6 @@
         send(sq_line, sq_line_in.at[d], z_send.at[nz - 1 + d], z_recv.at[nz - 1 + d], peer)
         for d, peer in enumerate(z_peers)
     ]
-    for hop in late_hops:
-        hop.wait_recv()
-    plane_sum(late_at)
-    base = z + slots + nz - slots * y
-    line_hops = [
-        send(
-            line.at[lax.rem(base + 1 + d, nz)], line_in.at[d], z_send.at[d], z_recv.at[d], peer
-        )
-        for d, peer in enumerate(z_peers)
-    ]
-
     def store_product(b, value):
         product[pl.ds(b * size, size), :] = value
 
@@ -389,13 +419,13 @@
     for d in range(nz - 1):
         norm = norm + sq_line_in[d]
     scale_out[...] = lax.rsqrt(norm / vertices)
-    for hop in line_hops:
-        hop.wait_recv()
-    value = line[lax.rem(base, nz)]
+    for copy in line_copies:
+        copy.wait_recv()
+    value = line[slot_of[0]]
     for d in range(nz - 1):
         value = value + line_in[d]
     gram_out[...] = value / vertices
-    for copy in started:
+    for copy in started + line_copies:
         copy.wait_send()
 
 
@@ -455,7 +485,7 @@
             pltpu.VMEM((rows, width), F32),
             pltpu.VMEM((rows, 2 * width), BF16),
             pltpu.VMEM(stiff_blocks.shape, BF16),
-            pltpu.VMEM((ny * width, width), BF16),
+            pltpu.VMEM(((ny + 1) * width, width), BF16),
             pltpu.VMEM((ny, 2, width, width), F32),
             pltpu.VMEM((nq, nz, 2, 4, width), F32),
             pltpu.VMEM((nq - 1, nz, 2, 4, width), F32),
@@ -466,13 +496,13 @@
             pltpu.VMEM((1, width), F32),
             pltpu.VMEM((nz - 1, 1, width), F32),
             pltpu.SemaphoreType.REGULAR((3,)),
-            dma((3 + ny,)),
+            dma((4 + ny,)),
             dma((4 + 2 * parts,)),
             dma((4 + 2 * parts,)),
             dma((6,)),
             dma((6,)),
-            dma((3 * (nq - 1),)),
-            dma((3 * (nq - 1),)),
+            dma((5 * (nq - 1),)),
+            dma((5 * (nq - 1),)),
             dma((2 * (nz - 1),)),
             dma((2 * (nz - 1),)),
         ],

time: 56.8 us -> 54.1 us (0.952)
  Pallas kernels: 56 us -> 53.3 us
    pallas_call x1, Pallas kernels: 54.2 us -> 51.6 us  [body(): pl.pallas_call(functools.partial(kernel, sizes), out_shape=(jax.ShapeDtyp...]
where the time goes in v4:
time: 54.1 us; the launch traced here: 54 us
  Pallas kernels  53.3 us (99%)
  between operations  0.64 us (1%)
    pallas_call x1, Pallas kernels, body(): pl.pallas_call(functools.partial(kernel, sizes), out_shape=(jax.ShapeDtyp...  51.6 us
    pallas_call x1, Pallas kernels, body(): pl.pallas_call(finish, out_shape=(jax.ShapeDtypeStruct((rows, width), BF1...  1.72 us

profile of v4, /device:TPU:1, one launch (start us, length us, event | category | flops | bytes accessed | tf_op | source)
XLA Modules:
  0.0 54.0 jit_solution(15050507922761814094)
XLA Ops:
  0.6 51.6 %shard_map.84 = (f32[2560,128]{1,0:T(8,128)S(1)}, f32[2560,128]{1,0:T(8,128)S(1)}, f32[1,128]{1,0:T(1,128)S(1)}, f32[2,4,128]{2,1,0:T(4,128)S(1)}) custom-call(s32[3,20]{1,0:T(4,128)} %bitcast.5, bf16[20,128,128]{2,1,0:T(8,128)(2,1)} %bitcast.3, bf16[20,3,128,128]{3,2,1,0:T(8,128)(2,1)} %blocks_ref.1, f32[20,128]{1,0:T(8,128)} %bitcast.4, ...), custom_call_target="tpu_custom_call" | custom-call | tf_op jit(solution)/shard_map/pallas_call | solution.py:470
  52.2 1.7 %shard_map.85 = (bf16[2560,128]{1,0:T(8,128)(2,1)}, bf16[2560,128]{1,0:T(8,128)(2,1)}, f32[4,128]{1,0:T(4,128)}, f32[4,128]{1,0:T(4,128)}) custom-call(f32[2560,128]{1,0:T(8,128)S(1)} %get-tuple-element.8.turned, f32[2560,128]{1,0:T(8,128)S(1)} %get-tuple-element.9.product, f32[1,128]{1,0:T(1,128)S(1)} %get-tuple-element.10.scale, ...), custom_call_target="tpu_custom_call" | custom-call | tf_op jit(solution)/shard_map/pallas_call | solution.py:519

commit v5 on v4

--- a/solution.py
+++ b/solution.py
@@ -24,7 +24,7 @@
 
 def kernel(
     sizes,
-    nb_ref,
+    nb_hbm,
     basis_ref,
     blocks_ref,
     mass_hbm,
@@ -36,6 +36,7 @@
     padded,
     others,
     rimmed,
+    nb_ref,
     mass_ref,
     mass_col,
     weights,
@@ -61,11 +62,12 @@
     z_send,
     z_recv,
 ):
-    nz, nx, ny, count, size, width, parts = sizes
+    nz, nx, ny, count, size, width, pieces = sizes
     z, x, k = (lax.axis_index(a) for a in ROWS)
     y = lax.axis_index("cols")
     half = count // 2
-    piece = half // parts
+    parts = len(pieces)
+    begins = [sum(pieces[:i]) for i in range(parts)]
     total = nz * nx * 2
     nq = 2 * nx
     q = 2 * x + k
@@ -99,6 +101,8 @@
     load_basis.start()
     load_mass = pltpu.make_async_copy(mass_hbm, mass_ref, load_sem.at[3 + ny])
     load_mass.start()
+    load_nb = pltpu.make_async_copy(nb_hbm, nb_ref, load_sem.at[4 + ny])
+    load_nb.start()
 
     peers = [y_right, y_left, partner, *x_near, *z_near]
     barrier = pltpu.get_barrier_semaphore()
@@ -206,6 +210,7 @@
         weights[pl.ds(b * size, size), :width] = value.astype(BF16)
 
     load_blocks.wait()
+    load_nb.wait()
     halo_low.wait_recv()
     halo_high.wait_recv()
     apply(padded, store_image)
@@ -259,14 +264,14 @@
     chunks = []
     far_low, far_high = [], []
     for i in range(parts):
-        starts = (i * piece, count - (i + 1) * piece)
+        starts = (begins[i], count - begins[i] - pieces[i])
         chunks.append(starts)
-        at = pl.ds(starts[0], piece)
+        at = pl.ds(starts[0], pieces[i])
         j = 4 + i
         far_low.append(
             send(others.at[0, at], others.at[2, at], y_send.at[j], y_recv.at[j], y_right)
         )
-        at = pl.ds(starts[1], piece)
+        at = pl.ds(starts[1], pieces[i])
         j = 4 + parts + i
         far_high.append(
             send(others.at[1, at], others.at[2, at], y_send.at[j], y_recv.at[j], y_left)
@@ -301,7 +306,7 @@
 
     sums = jnp.zeros((8, width), F32)
 
-    def far_turn(start, sums):
+    def far_turn(start, piece, sums):
         at = pl.ds(start * size, piece * size)
         if start < half:
             pair, place_of = [some(right, start, piece), some(far, start, piece)], 2
@@ -342,7 +347,8 @@
 
     def far_gram(i):
         for j, start in enumerate(chunks[i]):
-            add_gram(FAR, some(far, start, piece), start, piece, i == 0 and j == 0)
+            source = some(far, start, pieces[i])
+            add_gram(FAR, source, start, pieces[i], i == 0 and j == 0)
 
     slot_of = [lax.rem(z + d + slots + nz - slots * y, nz) for d in range(nz)]
     line_copies = [
@@ -362,16 +368,12 @@
         far_low[i].wait_recv()
         far_high[i].wait_recv()
         for start in chunks[i]:
-            sums = far_turn(start, sums)
-        if (i + 1) * piece % quarter == 0 and (i + 1) * piece <= BAND:
-            send_rims((i + 1) * piece)
+            sums = far_turn(start, pieces[i], sums)
+        done = begins[i] + pieces[i]
+        if done in (quarter, BAND):
+            send_rims(done)
         far_gram(i)
     early_at, late_at = pl.ds(0, early), pl.ds(early, slots)
-    for hop in early_hops:
-        hop.wait_recv()
-    plane_sum(early_at)
-    for d in far_first:
-        pl.when(slot_of[d + 1] < early)(line_copies[d].start)
     last = parts - 1
     far_low[last].wait_recv()
     far_high[last].wait_recv()
@@ -379,7 +381,7 @@
     pack(FAR)
     late_hops = plane_sends(late_at, 3 * (nq - 1))
     for start in chunks[last]:
-        sums = far_turn(start, sums)
+        sums = far_turn(start, pieces[last], sums)
     sq_own[...] = jnp.sum(sums, axis=0, keepdims=True)
     sq_hops = [
         send(
@@ -391,11 +393,11 @@
         )
         for d, peer in enumerate(q_peers)
     ]
-    for hop in late_hops:
+    for hop in early_hops:
         hop.wait_recv()
-    plane_sum(late_at)
+    plane_sum(early_at)
     for d in far_first:
-        pl.when(slot_of[d + 1] >= early)(line_copies[d].start)
+        pl.when(slot_of[d + 1] < early)(line_copies[d].start)
     for hop in sq_hops:
         hop.wait_recv()
     value = sq_own[...]
@@ -406,6 +408,12 @@
         send(sq_line, sq_line_in.at[d], z_send.at[nz - 1 + d], z_recv.at[nz - 1 + d], peer)
         for d, peer in enumerate(z_peers)
     ]
+    for hop in late_hops:
+        hop.wait_recv()
+    plane_sum(late_at)
+    for d in far_first:
+        pl.when(slot_of[d + 1] >= early)(line_copies[d].start)
+
     def store_product(b, value):
         product[pl.ds(b * size, size), :] = value
 
@@ -460,9 +468,10 @@
     ny = lax.axis_size("cols")
     rows, width = basis_rows.shape
     count, _, size, _ = stiff_blocks.shape
-    parts = 5
+    pieces = (2, 2, 2, 2, 1, 1)
+    parts = len(pieces)
     nq = 2 * nx
-    sizes = (nz, nx, ny, count, size, width, parts)
+    sizes = (nz, nx, ny, count, size, width, pieces)
     reach = (count + 2 * BAND, size, width)
     vmem = pl.BlockSpec(memory_space=pltpu.VMEM)
     hbm = pl.BlockSpec(memory_space=pltpu.HBM)
@@ -475,12 +484,13 @@
             jax.ShapeDtypeStruct((1, width), F32),
             jax.ShapeDtypeStruct((2, 4, width), F32),
         ),
-        in_specs=[pl.BlockSpec(memory_space=pltpu.SMEM), hbm, hbm, hbm, hbm],
+        in_specs=[hbm] * 5,
         out_specs=(vmem, vmem, vmem, vmem),
         scratch_shapes=[
             pltpu.VMEM(reach, BF16),
             pltpu.VMEM((3, count, size, width), BF16),
             pltpu.VMEM(reach, BF16),
+            pltpu.SMEM((3, count), jnp.int32),
             pltpu.VMEM((count, size), F32),
             pltpu.VMEM((rows, width), F32),
             pltpu.VMEM((rows, 2 * width), BF16),
@@ -496,7 +506,7 @@
             pltpu.VMEM((1, width), F32),
             pltpu.VMEM((nz - 1, 1, width), F32),
             pltpu.SemaphoreType.REGULAR((3,)),
-            dma((4 + ny,)),
+            dma((5 + ny,)),
             dma((4 + 2 * parts,)),
             dma((4 + 2 * parts,)),
             dma((6,)),

time: 54.1 us -> 52.3 us (0.967)
  Pallas kernels: 53.3 us -> 51.5 us
    pallas_call x1, Pallas kernels: 51.6 us -> 49.8 us  [body(): pl.pallas_call(functools.partial(kernel, sizes), out_shape=(jax.ShapeDtyp...]
where the time goes in v5:
time: 52.3 us; the launch traced here: 52.2 us
  Pallas kernels  51.5 us (98%)
  between operations  0.64 us (1%)
    pallas_call x1, Pallas kernels, body(): pl.pallas_call(functools.partial(kernel, sizes), out_shape=(jax.ShapeDtyp...  49.8 us
    pallas_call x1, Pallas kernels, body(): pl.pallas_call(finish, out_shape=(jax.ShapeDtypeStruct((rows, width), BF1...  1.72 us

profile of v5, /device:TPU:1, one launch (start us, length us, event | category | flops | bytes accessed | tf_op | source)
XLA Modules:
  0.0 52.2 jit_solution(16946906088208112033)
XLA Ops:
  0.6 49.8 %shard_map.84 = (f32[2560,128]{1,0:T(8,128)S(1)}, f32[2560,128]{1,0:T(8,128)S(1)}, f32[1,128]{1,0:T(1,128)S(1)}, f32[2,4,128]{2,1,0:T(4,128)S(1)}) custom-call(s32[3,20]{1,0:T(4,128)} %bitcast.5, bf16[20,128,128]{2,1,0:T(8,128)(2,1)} %bitcast.3, bf16[20,3,128,128]{3,2,1,0:T(8,128)(2,1)} %blocks_ref.1, f32[20,128]{1,0:T(8,128)} %bitcast.4, ...), custom_call_target="tpu_custom_call" | custom-call | tf_op jit(solution)/shard_map/pallas_call | solution.py:479
  50.5 1.7 %shard_map.85 = (bf16[2560,128]{1,0:T(8,128)(2,1)}, bf16[2560,128]{1,0:T(8,128)(2,1)}, f32[4,128]{1,0:T(4,128)}, f32[4,128]{1,0:T(4,128)}) custom-call(f32[2560,128]{1,0:T(8,128)S(1)} %get-tuple-element.8.turned, f32[2560,128]{1,0:T(8,128)S(1)} %get-tuple-element.9.product, f32[1,128]{1,0:T(1,128)S(1)} %get-tuple-element.10.scale, ...), custom_call_target="tpu_custom_call" | custom-call | tf_op jit(solution)/shard_map/pallas_call | solution.py:529

commit v6 on v5

--- a/solution.py
+++ b/solution.py
@@ -225,10 +225,6 @@
     def some(ref, start, length):
         return ref[pl.ds(start, length)].reshape(length * size, width)
 
-    step = count // 4
-    for i in range(4):
-        add_gram(OWN, some(padded, BAND + i * step, step), i * step, step, i == 0)
-
     def pack(which):
         for t in range(width // 8):
             for j in range(2):
@@ -256,9 +252,6 @@
         line[at] = value
 
     at_piece = [pl.ds(slots * i, slots) for i in range(ny)]
-    pack(OWN)
-    early_hops = plane_sends(at_piece[OWN], 0)
-
     left_first.wait_recv()
     right_first.wait_recv()
     chunks = []
@@ -277,6 +270,12 @@
             send(others.at[1, at], others.at[2, at], y_send.at[j], y_recv.at[j], y_left)
         )
     left, right, far = (others.at[i] for i in range(3))
+    step = count // 4
+    for i in range(4):
+        add_gram(OWN, some(padded, BAND + i * step, step), i * step, step, i == 0)
+
+    pack(OWN)
+    early_hops = plane_sends(at_piece[OWN], 0)
     for i in range(2):
         add_gram(LEFT, some(left, i * step, step), i * step, step, i == 0)
     for i in range(2, 4):
@@ -369,9 +368,8 @@
         far_high[i].wait_recv()
         for start in chunks[i]:
             sums = far_turn(start, pieces[i], sums)
-        done = begins[i] + pieces[i]
-        if done in (quarter, BAND):
-            send_rims(done)
+        if begins[i] + pieces[i] == quarter:
+            send_rims(quarter)
         far_gram(i)
     early_at, late_at = pl.ds(0, early), pl.ds(early, slots)
     last = parts - 1
@@ -393,6 +391,7 @@
         )
         for d, peer in enumerate(q_peers)
     ]
+    send_rims(BAND)
     for hop in early_hops:
         hop.wait_recv()
     plane_sum(early_at)

time: 52.3 us -> 53.3 us (1.019)
  Pallas kernels: 51.5 us -> 52.5 us
    pallas_call x1, Pallas kernels: 49.8 us -> 50.8 us  [body(): pl.pallas_call(functools.partial(kernel, sizes), out_shape=(jax.ShapeDtyp...]
where the time goes in v6:
time: 53.3 us; the launch traced here: 53.2 us
  Pallas kernels  52.5 us (98%)
  between operations  0.64 us (1%)
    pallas_call x1, Pallas kernels, body(): pl.pallas_call(functools.partial(kernel, sizes), out_shape=(jax.ShapeDtyp...  50.8 us
    pallas_call x1, Pallas kernels, body(): pl.pallas_call(finish, out_shape=(jax.ShapeDtypeStruct((rows, width), BF1...  1.72 us

profile of v6, /device:TPU:1, one launch (start us, length us, event | category | flops | bytes accessed | tf_op | source)
XLA Modules:
  0.0 53.2 jit_solution(2771891287716144436)
XLA Ops:
  0.6 50.8 %shard_map.84 = (f32[2560,128]{1,0:T(8,128)S(1)}, f32[2560,128]{1,0:T(8,128)S(1)}, f32[1,128]{1,0:T(1,128)S(1)}, f32[2,4,128]{2,1,0:T(4,128)S(1)}) custom-call(s32[3,20]{1,0:T(4,128)} %bitcast.5, bf16[20,128,128]{2,1,0:T(8,128)(2,1)} %bitcast.3, bf16[20,3,128,128]{3,2,1,0:T(8,128)(2,1)} %blocks_ref.1, f32[20,128]{1,0:T(8,128)} %bitcast.4, ...), custom_call_target="tpu_custom_call" | custom-call | tf_op jit(solution)/shard_map/pallas_call | solution.py:478
  51.4 1.7 %shard_map.85 = (bf16[2560,128]{1,0:T(8,128)(2,1)}, bf16[2560,128]{1,0:T(8,128)(2,1)}, f32[4,128]{1,0:T(4,128)}, f32[4,128]{1,0:T(4,128)}) custom-call(f32[2560,128]{1,0:T(8,128)S(1)} %get-tuple-element.8.turned, f32[2560,128]{1,0:T(8,128)S(1)} %get-tuple-element.9.product, f32[1,128]{1,0:T(1,128)S(1)} %get-tuple-element.10.scale, ...), custom_call_target="tpu_custom_call" | custom-call | tf_op jit(solution)/shard_map/pallas_call | solution.py:528

commit v7 on v6

--- a/solution.py
+++ b/solution.py
@@ -227,11 +227,12 @@
 
     def pack(which):
         for t in range(width // 8):
-            for j in range(2):
-                value = gram[which, j, pl.ds(8 * t, 8), :]
-                at = slots * which + t // nx
-                plane[2 * (t % nx), at, j] = value[:4]
-                plane[2 * (t % nx) + 1, at, j] = value[4:]
+            stiff, mass = (gram[which, j, pl.ds(8 * t, 8), :] for j in range(2))
+            at = slots * which + t // nx
+            for c in range(2):
+                rows = slice(4 * c, 4 * c + 4)
+                both = jnp.concatenate([stiff[rows], mass[rows]], axis=0)
+                plane[2 * (t % nx) + c, at] = both.astype(BF16)
 
     def plane_sends(at, offset):
         return [
@@ -246,9 +247,9 @@
         ]
 
     def plane_sum(at):
-        value = plane[q, at]
+        value = plane[q, at].astype(F32)
         for d in range(nq - 1):
-            value = value + plane_in[d, at]
+            value = value + plane_in[d, at].astype(F32)
         line[at] = value
 
     at_piece = [pl.ds(slots * i, slots) for i in range(ny)]
@@ -368,8 +369,9 @@
         far_high[i].wait_recv()
         for start in chunks[i]:
             sums = far_turn(start, pieces[i], sums)
-        if begins[i] + pieces[i] == quarter:
-            send_rims(quarter)
+        done = begins[i] + pieces[i]
+        if done in (quarter, BAND):
+            send_rims(done)
         far_gram(i)
     early_at, late_at = pl.ds(0, early), pl.ds(early, slots)
     last = parts - 1
@@ -391,7 +393,6 @@
         )
         for d, peer in enumerate(q_peers)
     ]
-    send_rims(BAND)
     for hop in early_hops:
         hop.wait_recv()
     plane_sum(early_at)
@@ -443,8 +444,8 @@
     pieces = 4
     step = rows // pieces
     copies = []
-    stiff_out[...] = gram[0]
-    mass_out[...] = gram[1]
+    stiff_out[...] = gram[:4, :]
+    mass_out[...] = gram[4:, :]
     for i in range(pieces):
         at = pl.ds(i * step, step)
         for j, (source, held, target) in enumerate(
@@ -481,7 +482,7 @@
             jax.ShapeDtypeStruct((rows, width), F32),
             jax.ShapeDtypeStruct((rows, width), F32),
             jax.ShapeDtypeStruct((1, width), F32),
-            jax.ShapeDtypeStruct((2, 4, width), F32),
+            jax.ShapeDtypeStruct((8, width), F32),
         ),
         in_specs=[hbm] * 5,
         out_specs=(vmem, vmem, vmem, vmem),
@@ -496,10 +497,10 @@
             pltpu.VMEM(stiff_blocks.shape, BF16),
             pltpu.VMEM(((ny + 1) * width, width), BF16),
             pltpu.VMEM((ny, 2, width, width), F32),
-            pltpu.VMEM((nq, nz, 2, 4, width), F32),
-            pltpu.VMEM((nq - 1, nz, 2, 4, width), F32),
-            pltpu.VMEM((nz, 2, 4, width), F32),
-            pltpu.VMEM((nz - 1, 2, 4, width), F32),
+            pltpu.VMEM((nq, nz, 8, width), BF16),
+            pltpu.VMEM((nq - 1, nz, 8, width), BF16),
+            pltpu.VMEM((nz, 8, width), F32),
+            pltpu.VMEM((nz - 1, 8, width), F32),
             pltpu.VMEM((1, width), F32),
             pltpu.VMEM((nq - 1, 1, width), F32),
             pltpu.VMEM((1, width), F32),

time: 53.3 us -> 51.9 us (0.974)
  Pallas kernels: 52.5 us -> 51.1 us
    pallas_call x1, Pallas kernels: 50.8 us -> 49.4 us  [body(): pl.pallas_call(functools.partial(kernel, sizes), out_shape=(jax.ShapeDtyp...]
where the time goes in v7:
time: 51.9 us; the launch traced here: 51.8 us
  Pallas kernels  51.1 us (98%)
  between operations  0.64 us (1%)
    pallas_call x1, Pallas kernels, body(): pl.pallas_call(functools.partial(kernel, sizes), out_shape=(jax.ShapeDtyp...  49.4 us
    pallas_call x1, Pallas kernels, body(): pl.pallas_call(finish, out_shape=(jax.ShapeDtypeStruct((rows, width), BF1...  1.72 us

profile of v7, /device:TPU:1, one launch (start us, length us, event | category | flops | bytes accessed | tf_op | source)
XLA Modules:
  0.0 51.8 jit_solution(6338315881212228523)
XLA Ops:
  0.6 49.4 %shard_map.84 = (f32[2560,128]{1,0:T(8,128)S(1)}, f32[2560,128]{1,0:T(8,128)S(1)}, f32[1,128]{1,0:T(1,128)S(1)}, f32[8,128]{1,0:T(8,128)S(1)}) custom-call(s32[3,20]{1,0:T(4,128)} %bitcast.5, bf16[20,128,128]{2,1,0:T(8,128)(2,1)} %bitcast.3, bf16[20,3,128,128]{3,2,1,0:T(8,128)(2,1)} %blocks_ref.1, f32[20,128]{1,0:T(8,128)} %bitcast.4, bf16[512,512]{1,0:T(8,128)(2,1)} %rot_ref.1), custom_call_target="tpu_custom_call" | custom-call | tf_op jit(solution)/shard_map/pallas_call | solution.py:479
  50.1 1.7 %shard_map.85 = (bf16[2560,128]{1,0:T(8,128)(2,1)}, bf16[2560,128]{1,0:T(8,128)(2,1)}, f32[4,128]{1,0:T(4,128)}, f32[4,128]{1,0:T(4,128)}) custom-call(f32[2560,128]{1,0:T(8,128)S(1)} %get-tuple-element.8.turned, f32[2560,128]{1,0:T(8,128)S(1)} %get-tuple-element.9.product, f32[1,128]{1,0:T(1,128)S(1)} %get-tuple-element.10.scale, ...), custom_call_target="tpu_custom_call" | custom-call | tf_op jit(solution)/shard_map/pallas_call | solution.py:529

commit v8 on v7

--- a/solution.py
+++ b/solution.py
@@ -97,8 +97,15 @@
     z_peers = [along("rows_0", z, nz, d) for d in range(1, nz)]
     col_of = [lax.rem(y + ny - 1 + i, ny) for i in range(ny)]
 
-    load_basis = pltpu.make_async_copy(basis_ref, padded.at[pl.ds(BAND, count)], load_sem.at[0])
-    load_basis.start()
+    load_basis = []
+    for i in range(2):
+        load = pltpu.make_async_copy(
+            basis_ref.at[pl.ds(i * half, half)],
+            padded.at[pl.ds(BAND + i * half, half)],
+            load_sem.at[5 * i + (ny if i else 0)],
+        )
+        load.start()
+        load_basis.append(load)
     load_mass = pltpu.make_async_copy(mass_hbm, mass_ref, load_sem.at[3 + ny])
     load_mass.start()
     load_nb = pltpu.make_async_copy(nb_hbm, nb_ref, load_sem.at[4 + ny])
@@ -122,7 +129,6 @@
         )
         load.start()
         load_turn.append(load)
-    load_basis.wait()
     pl.semaphore_wait(barrier, len(peers))
 
     started = []
@@ -142,9 +148,11 @@
 
     low, high = pl.ds(0, half), pl.ds(half, half)
     mine_low, mine_high = pl.ds(BAND, half), pl.ds(BAND + half, half)
+    load_basis[0].wait()
     left_first = send(
         padded.at[mine_low], others.at[0, low], y_send.at[0], y_recv.at[0], y_right
     )
+    load_basis[1].wait()
     right_first = send(
         padded.at[mine_high], others.at[1, high], y_send.at[1], y_recv.at[1], y_left
     )
@@ -468,7 +476,7 @@
     ny = lax.axis_size("cols")
     rows, width = basis_rows.shape
     count, _, size, _ = stiff_blocks.shape
-    pieces = (2, 2, 2, 2, 1, 1)
+    pieces = (4, 4, 1, 1)
     parts = len(pieces)
     nq = 2 * nx
     sizes = (nz, nx, ny, count, size, width, pieces)
@@ -506,7 +514,7 @@
             pltpu.VMEM((1, width), F32),
             pltpu.VMEM((nz - 1, 1, width), F32),
             pltpu.SemaphoreType.REGULAR((3,)),
-            dma((5 + ny,)),
+            dma((6 + ny,)),
             dma((4 + 2 * parts,)),
             dma((4 + 2 * parts,)),
             dma((6,)),

time: 51.9 us -> 51.6 us (level)
  no operation moved by 1% of the time
where the time goes in v8:
time: 51.6 us; the launch traced here: 51.5 us
  Pallas kernels  50.9 us (99%)
  between operations  0.64 us (1%)
    pallas_call x1, Pallas kernels, body(): pl.pallas_call(functools.partial(kernel, sizes), out_shape=(jax.ShapeDtyp...  49.1 us
    pallas_call x1, Pallas kernels, body(): pl.pallas_call(finish, out_shape=(jax.ShapeDtypeStruct((rows, width), BF1...  1.72 us

profile of v8, /device:TPU:1, one launch (start us, length us, event | category | flops | bytes accessed | tf_op | source)
XLA Modules:
  0.0 51.5 jit_solution(3566782843003799729)
XLA Ops:
  0.6 49.1 %shard_map.84 = (f32[2560,128]{1,0:T(8,128)S(1)}, f32[2560,128]{1,0:T(8,128)S(1)}, f32[1,128]{1,0:T(1,128)S(1)}, f32[8,128]{1,0:T(8,128)S(1)}) custom-call(s32[3,20]{1,0:T(4,128)} %bitcast.5, bf16[20,128,128]{2,1,0:T(8,128)(2,1)} %bitcast.3, bf16[20,3,128,128]{3,2,1,0:T(8,128)(2,1)} %blocks_ref.1, f32[20,128]{1,0:T(8,128)} %bitcast.4, bf16[512,512]{1,0:T(8,128)(2,1)} %rot_ref.1), custom_call_target="tpu_custom_call" | custom-call | tf_op jit(solution)/shard_map/pallas_call | solution.py:487
  49.8 1.7 %shard_map.85 = (bf16[2560,128]{1,0:T(8,128)(2,1)}, bf16[2560,128]{1,0:T(8,128)(2,1)}, f32[4,128]{1,0:T(4,128)}, f32[4,128]{1,0:T(4,128)}) custom-call(f32[2560,128]{1,0:T(8,128)S(1)} %get-tuple-element.8.turned, f32[2560,128]{1,0:T(8,128)S(1)} %get-tuple-element.9.product, f32[1,128]{1,0:T(1,128)S(1)} %get-tuple-element.10.scale, ...), custom_call_target="tpu_custom_call" | custom-call | tf_op jit(solution)/shard_map/pallas_call | solution.py:537

commit v9 on v8

--- a/solution.py
+++ b/solution.py
@@ -354,9 +354,15 @@
         )
 
     def far_gram(i):
-        for j, start in enumerate(chunks[i]):
-            source = some(far, start, pieces[i])
-            add_gram(FAR, source, start, pieces[i], i == 0 and j == 0)
+        length = pieces[i]
+        source = jnp.concatenate([some(far, start, length) for start in chunks[i]], axis=0)
+        right_side = jnp.concatenate(
+            [weights[pl.ds(start * size, length * size), :] for start in chunks[i]], axis=0
+        )
+        part = transposed_dot(source, right_side)
+        for j in range(2):
+            value = part[:, j * width : (j + 1) * width]
+            gram[FAR, j] = value if i == 0 else gram[FAR, j] + value
 
     slot_of = [lax.rem(z + d + slots + nz - slots * y, nz) for d in range(nz)]
     line_copies = [

time: 51.6 us -> 51.6 us (level)
  no operation moved by 1% of the time
where the time goes in v9:
time: 51.6 us; the launch traced here: 51.5 us
  Pallas kernels  50.8 us (98%)
  between operations  0.64 us (1%)
    pallas_call x1, Pallas kernels, body(): pl.pallas_call(functools.partial(kernel, sizes), out_shape=(jax.ShapeDtyp...  49.1 us
    pallas_call x1, Pallas kernels, body(): pl.pallas_call(finish, out_shape=(jax.ShapeDtypeStruct((rows, width), BF1...  1.72 us

profile of v9, /device:TPU:1, one launch (start us, length us, event | category | flops | bytes accessed | tf_op | source)
XLA Modules:
  0.0 51.5 jit_solution(12531662105159932157)
XLA Ops:
  0.6 49.1 %shard_map.84 = (f32[2560,128]{1,0:T(8,128)S(1)}, f32[2560,128]{1,0:T(8,128)S(1)}, f32[1,128]{1,0:T(1,128)S(1)}, f32[8,128]{1,0:T(8,128)S(1)}) custom-call(s32[3,20]{1,0:T(4,128)} %bitcast.5, bf16[20,128,128]{2,1,0:T(8,128)(2,1)} %bitcast.3, bf16[20,3,128,128]{3,2,1,0:T(8,128)(2,1)} %blocks_ref.1, f32[20,128]{1,0:T(8,128)} %bitcast.4, bf16[512,512]{1,0:T(8,128)(2,1)} %rot_ref.1), custom_call_target="tpu_custom_call" | custom-call | tf_op jit(solution)/shard_map/pallas_call | solution.py:493
  49.7 1.7 %shard_map.85 = (bf16[2560,128]{1,0:T(8,128)(2,1)}, bf16[2560,128]{1,0:T(8,128)(2,1)}, f32[4,128]{1,0:T(4,128)}, f32[4,128]{1,0:T(4,128)}) custom-call(f32[2560,128]{1,0:T(8,128)S(1)} %get-tuple-element.8.turned, f32[2560,128]{1,0:T(8,128)S(1)} %get-tuple-element.9.product, f32[1,128]{1,0:T(1,128)S(1)} %get-tuple-element.10.scale, ...), custom_call_target="tpu_custom_call" | custom-call | tf_op jit(solution)/shard_map/pallas_call | solution.py:543
